TPU v7x, 32 devices: a whole 2x2x4 slice. The times are simulated.
32 devices in a mesh: views: 2 (over core), rows: 8 (over z, x), chan: 2 (over y).
Axes of the slice: x: 2, y: 2, z: 4, core: 2. Of those that a mesh axis runs over, the one named last changes fastest.
Arguments:
- latent: bfloat16 [32, 384, 256], P(('views', 'rows'), 'chan'), parts along dimension 0, may hold values from -6 to 6
- cache_low_a: bfloat16 [2, 32, 384, 256], P(None, ('views', 'rows'), 'chan'), parts along dimension 1, may hold values from -6 to 6
- cache_low_b: bfloat16 [2, 32, 384, 256], P(None, ('views', 'rows'), 'chan'), parts along dimension 1, may hold values from -6 to 6
- gain_low_a: bfloat16 [384], P('chan'), may hold values from 0.5 to 1.5
- gain_low_b: bfloat16 [384], P('chan'), may hold values from 0.5 to 1.5
- kernel_low_a: bfloat16 [3, 3, 3, 384, 384], P(None, None, None, 'chan'), may hold values from -0.0625 to 0.0625
- kernel_low_b: bfloat16 [3, 3, 3, 384, 384], P(None, None, None, 'chan'), may hold values from -0.0625 to 0.0625
- resample_kernel: bfloat16 [3, 3, 192, 384], P(None, None, 'rows'), may hold values from -0.109375 to 0.109375
- gain_high_a: bfloat16 [192], replicated, may hold values from 0.5 to 1.5
- gain_high_b: bfloat16 [192], replicated, may hold values from 0.5 to 1.5
- kernel_high_a: bfloat16 [3, 3, 3, 192, 192], P(None, None, None, 'rows'), may hold values from -0.078125 to 0.078125
- kernel_high_b: bfloat16 [3, 3, 3, 192, 192], P(None, None, None, 'rows'), may hold values from -0.078125 to 0.078125
- cache_high_a: bfloat16 [2, 64, 192, 512], P(None, ('views', 'rows'), None, 'chan'), parts along dimension 1, may hold values from -6 to 6
- cache_high_b: bfloat16 [2, 64, 192, 512], P(None, ('views', 'rows'), None, 'chan'), parts along dimension 1, may hold values from -6 to 6
Outputs:
- decoded: bfloat16 [64, 192, 512], P(('views', 'rows'), None, 'chan'), parts along dimension 0
There are 2 independent parts, one for each index of `views`. A program takes and returns all parts, laid end to end along the dimension named above; an argument that names none is the same for every part. Nothing has to cross between parts.
All inputs are finite; a program needn't handle non-finite values.
Results may differ from a plain program's by a relative error of at most 0.0095.
Values may be sent and summed in bfloat16 or wider, within the bound.
No kernel may reach another device: no remote copies, remote signals or barrier semaphores. Data moves between devices by JAX's collectives and lax.ppermute only.
A program may use at most 128 MiB of HBM per device.

v0:
```python
import functools

import jax
import jax.numpy as jnp
from jax import lax
from jax.experimental import pallas as pl
from jax.experimental.pallas import tpu as pltpu
from jax.sharding import PartitionSpec as P

F32, BF16 = jnp.float32, jnp.bfloat16
GRANT = 56 * 1024 * 1024


def in_vmem(*shape):
    return pl.BlockSpec(shape, lambda *_: (0,) * len(shape))


SCALAR = pl.BlockSpec(memory_space=pltpu.SMEM)


def call(body, name, args, specs, outs, scratch, flops, grid=()):
    moved = sum(a.size * a.dtype.itemsize for a in args) + sum(
        o.size * o.dtype.itemsize for o in outs
    )
    return pl.pallas_call(
        body,
        name=name,
        grid=grid,
        in_specs=specs,
        out_specs=[in_vmem(*o.shape) for o in outs],
        out_shape=outs,
        scratch_shapes=scratch,
        compiler_params=pltpu.CompilerParams(vmem_limit_bytes=GRANT),
        cost_estimate=pl.CostEstimate(flops=flops, bytes_accessed=moved, transcendentals=0),
    )(*args)


def activated(values, gain):
    mean = jnp.mean(values * values, axis=0, keepdims=True)
    scaled = values * lax.rsqrt(mean + 1e-06) * gain
    return scaled / (1.0 + jnp.exp(-scaled))


def rolled(value, step):
    count = value.shape[1]
    return value if step == 0 else pltpu.roll(value, step % count, 1)


def spread(columns, base, value, width, edged):
    depth, count = value.shape
    lane = lax.broadcasted_iota(jnp.int32, value.shape, 1)
    for j in range(3):
        moved = rolled(value, 1 - j)
        if edged and j == 0:
            moved = jnp.where(lane == 0, 0.0, moved)
        if edged and j == 2:
            moved = jnp.where(lane == count - 1, 0.0, moved)
        columns[base + j * depth : base + (j + 1) * depth, :] = moved[:, :width].astype(BF16)


def joined(c, own, other, whole):
    half = own.shape[0]
    whole[pl.ds(pl.multiple_of(c * half, half), half), :] = own.astype(F32)
    whole[pl.ds(pl.multiple_of((1 - c) * half, half), half), :] = other.astype(F32)
    return whole[...]


def low_cached_body(place, own, other, weights, total, columns, whole):
    frames, rows, half, _ = own.shape
    outs, depth = weights.shape[3:]
    total[...] = jnp.zeros_like(total)

    def row(r, _):
        for t in range(frames):
            value = joined(place[0], own[t, r], other[t, r], whole)
            spread(columns, t * 3 * depth, value, value.shape[1], True)
        sums = None
        for t in range(frames):
            left = jnp.concatenate(
                [weights[t, :, j].reshape(3 * outs, depth) for j in range(3)], axis=1
            )
            part = jnp.dot(
                left, columns[t * 3 * depth : (t + 1) * 3 * depth, :], preferred_element_type=F32
            )
            sums = part if sums is None else sums + part
        for i in range(3):
            total[r + 2 - i] += sums[i * outs : (i + 1) * outs]
        return 0

    lax.fori_loop(0, rows, row, 0)


def low_living_body(place, own, other, gain, cached, weights, inner, edges, total, columns, whole):
    rows, half, _ = own.shape
    outs, depth = weights.shape[3:]
    total[...] = cached[...]

    def row(r, _):
        value = joined(place[0], own[r], other[r], whole)
        value = activated(value, gain[...])
        spread(columns, 0, value, value.shape[1], True)
        left = jnp.concatenate(
            [weights[0, :, j].reshape(3 * outs, depth) for j in range(3)], axis=1
        )
        sums = jnp.dot(left, columns[...], preferred_element_type=F32)
        for i in range(3):
            total[r + 2 - i] += sums[i * outs : (i + 1) * outs]
        return 0

    lax.fori_loop(0, rows, row, 0)
    inner[...] = total[1 : rows + 1]
    edges[0] = total[0].astype(BF16)
    edges[1] = total[rows + 1].astype(BF16)


def low_cached(place, own, other, kernel):
    frames, rows, half, width = own.shape
    outs, depth = kernel.shape[3:]
    return call(
        low_cached_body,
        "low_cached",
        (place, own, other, kernel),
        [
            SCALAR,
            in_vmem(*own.shape),
            in_vmem(*other.shape),
            in_vmem(frames, 3, 3, outs, depth),
        ],
        [jax.ShapeDtypeStruct((rows + 2, outs, width), F32)],
        [pltpu.VMEM((frames * 3 * depth, width), BF16), pltpu.VMEM((depth, width), F32)],
        2 * frames * 9 * outs * depth * rows * width,
        (1,),
    )[0]


def low_living(place, own, other, gain, cached, kernel):
    rows, half, width = own.shape
    frames = kernel.shape[0]
    outs, depth = kernel.shape[3:]
    return call(
        low_living_body,
        "low_living",
        (place, own, other, gain, cached, kernel),
        [
            SCALAR,
            in_vmem(*own.shape),
            in_vmem(*other.shape),
            in_vmem(*gain.shape),
            in_vmem(*cached.shape),
            pl.BlockSpec((1, 3, 3, outs, depth), lambda _: (frames - 1, 0, 0, 0, 0)),
        ],
        [
            jax.ShapeDtypeStruct((rows, outs, width), F32),
            jax.ShapeDtypeStruct((2, outs, width), BF16),
        ],
        [
            pltpu.VMEM((rows + 2, outs, width), F32),
            pltpu.VMEM((3 * depth, width), BF16),
            pltpu.VMEM((depth, width), F32),
        ],
        2 * 9 * outs * depth * rows * width,
        (1,),
    )


def high_sums(total, first, sums, outs, share):
    for i in range(3):
        for s in range(outs // share):
            total[first + 2 - i, s * share : (s + 1) * share, :] += sums[
                (3 * s + i) * share : (3 * s + i + 1) * share
            ]


def left_of(weights, pieces, first, last):
    rows, lanes = weights.shape[0] // pieces, weights.shape[1]
    parts = []
    while first < last:
        piece, start = divmod(first, lanes)
        stop = min(lanes, start + last - first)
        parts.append(weights[piece * rows : (piece + 1) * rows, start:stop])
        first += stop - start
    return parts[0] if len(parts) == 1 else jnp.concatenate(parts, axis=1)


def kept_lanes(c, width, shape):
    lane = lax.broadcasted_iota(jnp.int32, shape, 1)
    count = shape[1]
    middle = (width + count) // 2
    return (lane < jnp.where(c == 0, middle, width)) | (lane >= jnp.where(c == 0, count, middle))


def high_cached_body(
    share, place, own_a, strip_a, own_b, strip_b, weights, sums_a, sums_b, up, down,
    total_a, total_b, columns_a, columns_b, whole,
):
    frames, rows, depth, width = own_a.shape
    count = width + strip_a.shape[3]
    c = place[0]
    keep = kept_lanes(c, width, (depth, count))
    total_a[...] = jnp.zeros_like(total_a)
    total_b[...] = jnp.zeros_like(total_b)
    pieces = weights.shape[0] // (3 * depth)
    long = frames * 3 * depth
    second = long + 6 * depth

    def row(r, _):
        for own, strip, columns, upto in (
            (own_a, strip_a, columns_a, count),
            (own_b, strip_b, columns_b, width),
        ):
            for t in range(frames):
                whole[:, :width] = own[t, r].astype(F32)
                whole[:, width:] = strip[t, r].astype(F32)
                value = jnp.where(keep, whole[...], 0.0)
                spread(columns, t * 3 * depth, value, upto, False)
        part = jnp.dot(left_of(weights, pieces, 0, long), columns_a[...], preferred_element_type=F32)
        high_sums(total_a, r, part, depth, share)
        part = jnp.dot(
            left_of(weights, pieces, second, second + long),
            columns_b[...],
            preferred_element_type=F32,
        )
        high_sums(total_b, r, part, depth, share)
        return 0

    lax.fori_loop(0, rows, row, 0)
    sums_a[...] = total_a[...]
    sums_b[...] = total_b[1 : rows + 1]
    block = 128
    for packet, first, edge in ((up, 0, 0), (down, rows, rows + 1)):
        place_at = 0
        for source, at in ((total_a, first), (total_a, first + 1), (total_b, edge)):
            for lane in range(0, source.shape[2], block):
                packet[place_at] = source[at, :, lane : lane + block].astype(BF16)
                place_at += 1


def high_cached(place, own_a, strip_a, own_b, strip_b, weights, share):
    frames, rows, depth, width = own_a.shape
    count = width + strip_a.shape[3]
    blocks = (2 * count + width) // 128
    args = (place, own_a, strip_a, own_b, strip_b, weights)
    return call(
        functools.partial(high_cached_body, share),
        "high_cached",
        args,
        [SCALAR] + [in_vmem(*a.shape) for a in args[1:]],
        [
            jax.ShapeDtypeStruct((rows + 2, depth, count), F32),
            jax.ShapeDtypeStruct((rows, depth, width), F32),
            jax.ShapeDtypeStruct((blocks, depth, 128), BF16),
            jax.ShapeDtypeStruct((blocks, depth, 128), BF16),
        ],
        [
            pltpu.VMEM((rows + 2, depth, count), F32),
            pltpu.VMEM((rows + 2, depth, width), F32),
            pltpu.VMEM((frames * 3 * depth, count), BF16),
            pltpu.VMEM((frames * 3 * depth, width), BF16),
            pltpu.VMEM((depth, count), F32),
        ],
        2 * frames * 9 * depth * depth * rows * (width + count),
    )


def high_living_body(
    share, place, own, other, above, below, gain_a, gain_b, sums_a, sums_b, from_above, from_below,
    weights, decoded, wide, total, total_a, total_b, resampled, columns_r, columns, whole,
):
    rows, half, low_width = own.shape
    high_rows, outs, width = decoded.shape
    count = sums_a.shape[2]
    c, first, last = place[0], place[1], place[2]
    depth = 2 * half
    pieces = weights.shape[0] // (3 * outs)
    long = 6 * outs
    keep = kept_lanes(c, width, (outs, count))

    lane = lax.broadcasted_iota(jnp.int32, (low_width, count), 1)
    source = lax.broadcasted_iota(jnp.int32, (low_width, count), 0)
    column = jnp.where((c == 1) & (lane >= (width + count) // 2), lane - count, lane) + c * width
    wide[...] = jnp.where(kept_lanes(c, width, column.shape) & (column // 2 == source), 1.0, 0.0).astype(BF16)

    total[...] = jnp.zeros_like(total)

    def low_row(value, m):
        value = jnp.dot(value, wide[...], preferred_element_type=F32)
        spread(columns_r, 0, value, count, False)
        part = jnp.dot(
            left_of(weights, pieces, 3 * long, 3 * long + 3 * depth),
            columns_r[...],
            preferred_element_type=F32,
        )
        for s in range(outs // share):
            at = pl.ds(s * share, share)
            p0, p1, p2 = (
                part[(3 * s + i) * share : (3 * s + i + 1) * share] for i in range(3)
            )
            total[2 * m, at, :] += p2
            total[2 * m + 1, at, :] += p1 + p2
            total[2 * m + 2, at, :] += p0 + p1
            total[2 * m + 3, at, :] += p0

    def near(m, _):
        low_row(joined(c, own[m], other[m], whole).astype(BF16), m + rows)
        return 0

    def far(m, _):
        low_row(above[m], m)
        low_row(below[m], m + 2 * rows)
        return 0

    lax.fori_loop(0, rows, near, 0)
    lax.fori_loop(0, rows, far, 0)

    spare = 2 * rows - 1
    total_a[...] = jnp.zeros_like(total_a)
    total_a[2 : high_rows + 4] = sums_a[...]
    total_b[...] = jnp.zeros_like(total_b)
    total_b[2 : high_rows + 2] = sums_b[...]
    block = 128
    for packet, at_a, at_b in ((from_above, 2, 2), (from_below, high_rows + 2, high_rows + 1)):
        spot = 0
        for target, at in ((total_a, at_a), (total_a, at_a + 1), (total_b, at_b)):
            for start in range(0, target.shape[2], block):
                target[at, :, start : start + block] += packet[spot].astype(F32)
                spot += 1

    columns[...] = jnp.zeros_like(columns)
    pad = columns.shape[0] - 3 * outs

    def high_a(h, _):
        outside = ((first == 1) & (h < 2)) | ((last == 1) & (h >= high_rows + 2))
        value = jnp.where(keep, total[h + spare], 0.0).astype(BF16)
        value = jnp.where(outside, jnp.zeros_like(value), value)
        resampled[h] = value
        value = activated(value.astype(F32), gain_a[...])
        spread(columns, 0, value, count, False)
        part = jnp.dot(
            left_of(weights, pieces, long, long + columns.shape[0]), columns[...], preferred_element_type=F32
        )
        high_sums(total_a, h, part, outs, share)
        return 0

    lax.fori_loop(0, high_rows + 4, high_a, 0)
    columns[:pad, :] = jnp.zeros((pad, count), BF16)

    def high_b(h, _):
        outside = ((first == 1) & (h < 1)) | ((last == 1) & (h >= high_rows + 1))
        value = jnp.where(keep, total_a[h + 2], 0.0).astype(BF16)
        value = jnp.where(outside, jnp.zeros_like(value), value)
        value = activated(value.astype(F32), gain_b[...])
        for j in range(3):
            moved = rolled(value, 1 - j)
            columns[pad + j * outs : pad + (j + 1) * outs, :width] = moved[:, :width].astype(BF16)
        part = jnp.dot(
            left_of(weights, pieces, 2 * long - columns.shape[0], 2 * long),
            columns[:, :width],
            preferred_element_type=F32,
        )
        high_sums(total_b, h, part, outs, share)
        return 0

    lax.fori_loop(0, high_rows + 2, high_b, 0)
    for h in range(high_rows):
        decoded[h] = (total_b[h + 2] + resampled[h + 2, :, :width].astype(F32)).astype(BF16)


def high_living(
    place, own, other, above, below, gain_a, gain_b, sums_a, sums_b, from_above, from_below,
    weights, share,
):
    rows, half, low_width = own.shape
    high_rows, outs, width = sums_b.shape
    count = sums_a.shape[2]
    depth = 2 * half
    args = (
        place, own, other, above, below, gain_a, gain_b, sums_a, sums_b, from_above, from_below,
        weights,
    )
    padded = -(-3 * outs // 128) * 128
    return call(
        functools.partial(high_living_body, share),
        "high_living",
        args,
        [SCALAR] + [in_vmem(*a.shape) for a in args[1:]],
        [jax.ShapeDtypeStruct((high_rows, outs, width), BF16)],
        [
            pltpu.VMEM((low_width, count), BF16),
            pltpu.VMEM((6 * rows + 2, outs, count), F32),
            pltpu.VMEM((high_rows + 6, outs, count), F32),
            pltpu.VMEM((high_rows + 4, outs, width), F32),
            pltpu.VMEM((high_rows + 4, outs, count), BF16),
            pltpu.VMEM((3 * depth, count), BF16),
            pltpu.VMEM((padded, count), BF16),
            pltpu.VMEM((depth, low_width), F32),
        ],
        2 * 27 * outs * outs * high_rows * width + 2 * 9 * outs * depth * high_rows * count,
    )[0]


def body(
    latent,
    cache_low_a,
    cache_low_b,
    gain_low_a,
    gain_low_b,
    kernel_low_a,
    kernel_low_b,
    resample_kernel,
    gain_high_a,
    gain_high_b,
    kernel_high_a,
    kernel_high_b,
    cache_high_a,
    cache_high_b,
):
    c = lax.axis_index("chan")
    r = lax.axis_index("rows")
    row_count = lax.axis_size("rows")
    swap = [(0, 1), (1, 0)]

    def other_half(value):
        return lax.ppermute(value, "chan", swap)

    def downward(value):
        return lax.ppermute(value, "rows", [(i, i + 1) for i in range(row_count - 1)])

    def upward(value):
        return lax.ppermute(value, "rows", [(i + 1, i) for i in range(row_count - 1)])

    place = jnp.stack([c, r == 0, r == row_count - 1]).astype(jnp.int32)

    share = kernel_high_a.shape[3]

    def flat(kernel):
        turned = jnp.transpose(kernel, (1, 3, 0, 2, 4))
        return turned.reshape(3 * share, -1)

    flat_a, flat_b = flat(kernel_high_a), flat(kernel_high_b)
    flat_r = flat(resample_kernel[None])
    outs = kernel_high_a.shape[4]
    long = 6 * outs
    lined = jnp.concatenate([flat_a, flat_b[:, long:], flat_b[:, :long], flat_r], axis=1)
    pieces = lax.axis_size("views")
    lanes = -(-lined.shape[1] // (128 * pieces)) * 128
    lined = jnp.pad(lined, ((0, 0), (0, lanes * pieces - lined.shape[1])))
    mine = lax.dynamic_slice_in_dim(lined, lax.axis_index("views") * lanes, lanes, 1)
    weights = lax.all_gather(mine, ("views", "rows"), axis=0, tiled=True)
    if share % 8:
        weights = weights.reshape(pieces, -1, 3, share, lanes).transpose(0, 2, 1, 3, 4)
        weights = weights.reshape(-1, lanes)
        share = outs

    def column_of(gain, other):
        return jnp.where(
            c == 0, jnp.concatenate([gain, other]), jnp.concatenate([other, gain])
        ).astype(F32)[:, None]

    other_latent = other_half(latent)
    gains = jnp.stack([gain_low_a, gain_low_b])
    other_gains = other_half(gains)
    other_cache_a = other_half(cache_low_a)
    other_cache_b = other_half(cache_low_b)
    width = cache_high_a.shape[3]
    strip = 128
    edge = [
        lax.dynamic_slice_in_dim(cache, (1 - c) * (width - strip), strip, 3)
        for cache in (cache_high_a, cache_high_b)
    ]
    strips = other_half(jnp.stack(edge))

    def level1_conv(inputs, other, cached, gain, kernel):
        inner, edges = low_living(place, inputs, other, gain, cached, kernel)
        from_above = downward(edges[1])
        from_below = upward(edges[0])
        rest = jnp.zeros((inner.shape[0] - 2, *from_above.shape), BF16)
        added = jnp.concatenate([from_above[None], rest, from_below[None]])
        return inner + added.astype(F32)

    cached_a = low_cached(place, cache_low_a, other_cache_a, kernel_low_a)
    cached_b = low_cached(place, cache_low_b, other_cache_b, kernel_low_b)
    middle_low = level1_conv(
        latent, other_latent, cached_a, column_of(gains[0], other_gains[0]), kernel_low_a
    ).astype(BF16)
    level_one = (
        latent.astype(F32)
        + level1_conv(
            middle_low,
            other_half(middle_low),
            cached_b,
            column_of(gains[1], other_gains[1]),
            kernel_low_b,
        )
    ).astype(BF16)
    other_one = other_half(level_one)
    both = jnp.where(
        c == 0,
        jnp.concatenate([level_one, other_one], axis=1),
        jnp.concatenate([other_one, level_one], axis=1),
    )
    above, below = downward(both), upward(both)

    sums_a, sums_b, up, down = high_cached(
        place, cache_high_a, strips[0], cache_high_b, strips[1], weights, share
    )
    from_above, from_below = downward(down), upward(up)
    return high_living(
        place,
        level_one,
        other_one,
        above,
        below,
        gain_high_a.astype(F32)[:, None],
        gain_high_b.astype(F32)[:, None],
        sums_a,
        sums_b,
        from_above,
        from_below,
        weights,
        share,
    )


def solution(mesh):
    placed = (
        P(("views", "rows"), "chan", None),
        P(None, ("views", "rows"), "chan", None),
        P(None, ("views", "rows"), "chan", None),
        P("chan"),
        P("chan"),
        P(None, None, None, "chan", None),
        P(None, None, None, "chan", None),
        P(None, None, "rows", None),
        P(),
        P(),
        P(None, None, None, "rows", None),
        P(None, None, None, "rows", None),
        P(None, ("views", "rows"), None, "chan"),
        P(None, ("views", "rows"), None, "chan"),
    )
    return jax.shard_map(
        body,
        mesh=mesh,
        in_specs=placed,
        out_specs=P(("views", "rows"), None, "chan"),
        check_vma=False,
    )
```

profile of v0, /device:TPU:0, one launch (start us, length us, event | category | flops | bytes accessed | tf_op | source)
XLA Modules:
  0.0 151.6 jit_solution(16980196270641000644)
XLA Ops:
  6.6 1.2 copy.36
  8.2 1.1 copy.35
  9.6 1.0 copy.37
  12.2 3.1 %collective-permute-start.1 = (bf16[2,192]{1,0:T(2,128)(2,1)S(1)}, bf16[2,192]{1,0:T(2,128)(2,1)S(1)}, u32[]{:S(2)}, u32[]{:S(2)}) collective-permute-start(bf16[2,192]{1,0:T(2,128)(2,1)S(1)} %pad_maximum_fusion.5), channel_id=1, source_target_pairs={{0,1},{1,0},{2,3},{3,2},{4,5},{5,4},{6,7},{7,6},{8,9},{9,8},{10,11... | collective-permute-start | bytes 2312 | tf_op jit(solution)/shard_map/ppermute | solution.py:423
  15.3 1.9 %collective-permute-start = (bf16[2,192,256]{2,1,0:T(8,128)(2,1)S(1)}, bf16[2,192,256]{2,1,0:T(8,128)(2,1)S(1)}, u32[]{:S(2)}, u32[]{:S(2)}) collective-permute-start(bf16[2,192,256]{2,1,0:T(8,128)(2,1)S(1)} %copy-done.1), channel_id=1, source_target_pairs={{0,1},{1,0},{2,3},{3,2},{4,5},{5,4},{6,7},{7,6},{8,9},{9,8},{10,11... | collective-permute-start | bytes 589832 | tf_op jit(solution)/shard_map/ppermute | solution.py:423
  17.3 1.2 dynamic-slice_bitcast_fusion
  20.3 6.9 %collective-permute-done.2.other = bf16[2,2,192,256]{3,2,1,0:T(8,128)(2,1)S(1)} collective-permute-done((bf16[2,2,192,256]{3,2,1,0:T(8,128)(2,1)S(1)}, bf16[2,2,192,256]{3,2,1,0:T(8,128)(2,1)S(1)}, u32[]{:S(2)}, u32[]{:S(2)}) %collective-permute-start.2) | collective-permute-done | bytes 393248 | tf_op jit(solution)/shard_map/ppermute | solution.py:423
  28.0 5.2 %low_cached.2.cached = f32[4,192,256]{2,1,0:T(8,128)} custom-call(s32[3]{0:T(128)} %pad_add_fusion.place, bf16[2,2,192,256]{3,2,1,0:T(8,128)(2,1)} %own.3, bf16[2,2,192,256]{3,2,1,0:T(8,128)(2,1)} %copy-done.7, bf16[3,3,3,192,384]{4,3,2,1,0:T(8,128)(2,1)} %weights.5), custom_call_target="tpu_custom_call" | custom-call | flops 1358954496 | bytes 5554188 | tf_op jit(solution)/shard_map/low_cached/pallas_call | solution.py:25
  33.8 4.3 %low_living.2 = (f32[2,192,256]{2,1,0:T(8,128)}, bf16[2,192,256]{2,1,0:T(8,128)(2,1)}) custom-call(s32[3]{0:T(128)} %pad_add_fusion.place, bf16[2,192,256]{2,1,0:T(8,128)(2,1)} %own.4, bf16[2,192,256]{2,1,0:T(8,128)(2,1)} %copy-done.8, f32[384,1]{1,0:T(8,128)} %select_convert_fusion.1.gain, f32[4,192,256]{2,1,0:T(8,128)} %low_cached.2.cached, ...), custom_call_target="tpu_custom_call" | custom-call | flops 679477248 | bytes 5752332 | tf_op jit(solution)/shard_map/low_living/pallas_call | solution.py:25
  38.1 1.0 slice_bitcast_fusion.5
  39.1 3.4 %collective-permute-start.3 = (bf16[192,256]{1,0:T(8,128)(2,1)S(1)}, bf16[192,256]{1,0:T(8,128)(2,1)S(1)}, u32[]{:S(2)}, u32[]{:S(2)}) collective-permute-start(bf16[192,256]{1,0:T(8,128)(2,1)S(1)} %get-tuple-element.25), channel_id=1, source_target_pairs={{0,2},{2,4},{4,6},{6,8},{8,10},{10,12},{12,14},{1,3},{3,5},{5,7},{... | collective-permute-start | bytes 294920 | tf_op jit(solution)/shard_map/ppermute | solution.py:426
  42.5 1.3 collective-permute-start.4
  44.8 2.4 %collective-permute-done.3 = bf16[192,256]{1,0:T(8,128)(2,1)S(1)} collective-permute-done((bf16[192,256]{1,0:T(8,128)(2,1)S(1)}, bf16[192,256]{1,0:T(8,128)(2,1)S(1)}, u32[]{:S(2)}, u32[]{:S(2)}) %collective-permute-start.3) | collective-permute-done | bytes 98336 | tf_op jit(solution)/shard_map/ppermute | solution.py:426
  47.1 4.1 %collective-permute-done.4 = bf16[192,256]{1,0:T(8,128)(2,1)S(1)} collective-permute-done((bf16[192,256]{1,0:T(8,128)(2,1)S(1)}, bf16[192,256]{1,0:T(8,128)(2,1)S(1)}, u32[]{:S(2)}, u32[]{:S(2)}) %collective-permute-start.4) | collective-permute-done | bytes 98336 | tf_op jit(solution)/shard_map/ppermute | solution.py:429
  51.2 1.0 add_convert_fusion.1.own
  54.2 5.2 %low_cached.3.cached = f32[4,192,256]{2,1,0:T(8,128)} custom-call(s32[3]{0:T(128)} %pad_add_fusion.place, bf16[2,2,192,256]{3,2,1,0:T(8,128)(2,1)} %own.5, bf16[2,2,192,256]{3,2,1,0:T(8,128)(2,1)} %copy-done.6, bf16[3,3,3,192,384]{4,3,2,1,0:T(8,128)(2,1)} %weights.7), custom_call_target="tpu_custom_call" | custom-call | flops 1358954496 | bytes 5554188 | tf_op jit(solution)/shard_map/low_cached/pallas_call | solution.py:25
  59.4 5.1 %collective-permute-done.5.other = bf16[2,192,256]{2,1,0:T(8,128)(2,1)S(1)} collective-permute-done((bf16[2,192,256]{2,1,0:T(8,128)(2,1)S(1)}, bf16[2,192,256]{2,1,0:T(8,128)(2,1)S(1)}, u32[]{:S(2)}, u32[]{:S(2)}) %collective-permute-start.5) | collective-permute-done | bytes 196640 | tf_op jit(solution)/shard_map/ppermute | solution.py:423
  65.3 4.3 %low_living.3 = (f32[2,192,256]{2,1,0:T(8,128)}, bf16[2,192,256]{2,1,0:T(8,128)(2,1)}) custom-call(s32[3]{0:T(128)} %pad_add_fusion.place, bf16[2,192,256]{2,1,0:T(8,128)(2,1)} %copy-done, bf16[2,192,256]{2,1,0:T(8,128)(2,1)} %copy-done.9, f32[384,1]{1,0:T(8,128)} %select_convert_fusion.gain, f32[4,192,256]{2,1,0:T(8,128)} %low_cached.3.cached, ...), custom_call_target="tpu_custom_call" | custom-call | flops 679477248 | bytes 5752332 | tf_op jit(solution)/shard_map/low_living/pallas_call | solution.py:25
  69.5 1.0 slice_bitcast_fusion.3
  70.5 4.3 %collective-permute-start.7 = (bf16[192,256]{1,0:T(8,128)(2,1)S(1)}, bf16[192,256]{1,0:T(8,128)(2,1)S(1)}, u32[]{:S(2)}, u32[]{:S(2)}) collective-permute-start(bf16[192,256]{1,0:T(8,128)(2,1)S(1)} %get-tuple-element.23), channel_id=1, source_target_pairs={{0,2},{2,4},{4,6},{6,8},{8,10},{10,12},{12,14},{1,3},{3,5},{5,7},{... | collective-permute-start | bytes 294920 | tf_op jit(solution)/shard_map/ppermute | solution.py:426
  74.7 1.3 collective-permute-start.8
  76.0 1.8 %collective-permute-done.7 = bf16[192,256]{1,0:T(8,128)(2,1)S(1)} collective-permute-done((bf16[192,256]{1,0:T(8,128)(2,1)S(1)}, bf16[192,256]{1,0:T(8,128)(2,1)S(1)}, u32[]{:S(2)}, u32[]{:S(2)}) %collective-permute-start.7) | collective-permute-done | bytes 98336 | tf_op jit(solution)/shard_map/ppermute | solution.py:426
  77.8 4.0 %collective-permute-done.8 = bf16[192,256]{1,0:T(8,128)(2,1)S(1)} collective-permute-done((bf16[192,256]{1,0:T(8,128)(2,1)S(1)}, bf16[192,256]{1,0:T(8,128)(2,1)S(1)}, u32[]{:S(2)}, u32[]{:S(2)}) %collective-permute-start.8) | collective-permute-done | bytes 98336 | tf_op jit(solution)/shard_map/ppermute | solution.py:429
  81.8 1.1 add_convert_fusion.own
  84.4 4.2 %collective-permute-done.9.other = bf16[2,192,256]{2,1,0:T(8,128)(2,1)S(1)} collective-permute-done((bf16[2,192,256]{2,1,0:T(8,128)(2,1)S(1)}, bf16[2,192,256]{2,1,0:T(8,128)(2,1)S(1)}, u32[]{:S(2)}, u32[]{:S(2)}) %collective-permute-start.9) | collective-permute-done | bytes 196640 | tf_op jit(solution)/shard_map/ppermute | solution.py:423
  88.7 4.8 %collective-permute-start.10 = (bf16[2,384,256]{2,1,0:T(8,128)(2,1)S(1)}, bf16[2,384,256]{2,1,0:T(8,128)(2,1)S(1)}, u32[]{:S(2)}, u32[]{:S(2)}) collective-permute-start(bf16[2,384,256]{2,1,0:T(8,128)(2,1)S(1)} %maximum_select_fusion), channel_id=1, source_target_pairs={{0,2},{2,4},{4,6},{6,8},{8,10},{10,12},{12,14},{1,3},{3,5},{5,7},{... | collective-permute-start | bytes 1179656 | tf_op jit(solution)/shard_map/ppermute | solution.py:426
  93.6 1.3 collective-permute-start.11
  94.9 10.9 %high_cached.1 = (f32[6,192,384]{2,1,0:T(8,128)}, f32[4,192,256]{2,1,0:T(8,128)}, bf16[8,192,128]{2,1,0:T(8,128)(2,1)}, bf16[8,192,128]{2,1,0:T(8,128)(2,1)}) custom-call(s32[3]{0:T(128)} %pad_add_fusion.place, bf16[2,4,192,256]{3,2,1,0:T(8,128)(2,1)} %own_a.1, bf16[2,4,192,128]{3,2,1,0:T(8,128)(2,1)} %get-tuple-element.22.strip_a, ...), custom_call_target="tpu_custom_call" | custom-call | flops 3397386240 | bytes 11010060 | tf_op jit(solution)/shard_map/high_cached/pallas_call | solution.py:25
  105.9 4.6 %collective-permute-start.13 = (bf16[8,192,128]{2,1,0:T(8,128)(2,1)}, bf16[8,192,128]{2,1,0:T(8,128)(2,1)S(1)}, u32[]{:S(2)}, u32[]{:S(2)}) collective-permute-start(bf16[8,192,128]{2,1,0:T(8,128)(2,1)} %get-tuple-element.19), channel_id=1, source_target_pairs={{0,2},{2,4},{4,6},{6,8},{8,10},{10,12},{12,14},{1,3},{3,5},{5,7},{... | collective-permute-start | bytes 1179656 | tf_op jit(solution)/shard_map/ppermute | solution.py:426
  110.5 1.5 collective-permute-start.14
  113.5 7.3 %collective-permute-done.13.from_above = bf16[8,192,128]{2,1,0:T(8,128)(2,1)S(1)} collective-permute-done((bf16[8,192,128]{2,1,0:T(8,128)(2,1)}, bf16[8,192,128]{2,1,0:T(8,128)(2,1)S(1)}, u32[]{:S(2)}, u32[]{:S(2)}) %collective-permute-start.13) | collective-permute-done | bytes 393248 | tf_op jit(solution)/shard_map/ppermute | solution.py:426
  121.7 23.1 %high_living.1 = bf16[4,192,256]{2,1,0:T(8,128)(2,1)} custom-call(s32[3]{0:T(128)} %pad_add_fusion.place, bf16[2,192,256]{2,1,0:T(8,128)(2,1)} %copy-done.3, bf16[2,192,256]{2,1,0:T(8,128)(2,1)} %copy-done.10, bf16[2,384,256]{2,1,0:T(8,128)(2,1)} %copy-done.11, bf16[2,384,256]{2,1,0:T(8,128)(2,1)} %copy-done.12, f32[192,1]{1,0:T(8,128)} %copy.38.gain_a, ...), custom_call_target="tpu_custom_call" | custom-call | flops 4076863488 | bytes 10225164 | tf_op jit(solution)/shard_map/high_living/pallas_call | solution.py:25
  (81 shorter events, 13.3 us)
Async XLA Ops:
  6.5 5.6 %copy-start.15 = (bf16[192]{0:T(256)(128)(2,1)S(1)}, bf16[192]{0:T(256)(128)(2,1)}, u32[]{:S(2)}) copy-start(bf16[192]{0:T(256)(128)(2,1)} %param.17) | copy-start | bytes 1156
  6.5 5.6 %copy-start.16 = (bf16[192]{0:T(256)(128)(2,1)S(1)}, bf16[192]{0:T(256)(128)(2,1)}, u32[]{:S(2)}) copy-start(bf16[192]{0:T(256)(128)(2,1)} %param.18) | copy-start | bytes 1156
  6.5 8.7 %copy-start.4 = (bf16[2,2,192,256]{3,2,1,0:T(8,128)(2,1)S(1)}, bf16[2,2,192,256]{3,2,1,0:T(8,128)(2,1)}, u32[]{:S(2)}) copy-start(bf16[2,2,192,256]{3,2,1,0:T(8,128)(2,1)} %own.3) | copy-start | bytes 1179652
  6.5 8.8 %copy-start.1 = (bf16[2,192,256]{2,1,0:T(8,128)(2,1)S(1)}, bf16[2,192,256]{2,1,0:T(8,128)(2,1)}, u32[]{:S(2)}) copy-start(bf16[2,192,256]{2,1,0:T(8,128)(2,1)} %own.4) | copy-start | bytes 589828
  6.5 10.7 %copy-start.5 = (bf16[2,2,192,256]{3,2,1,0:T(8,128)(2,1)S(1)}, bf16[2,2,192,256]{3,2,1,0:T(8,128)(2,1)}, u32[]{:S(2)}) copy-start(bf16[2,2,192,256]{3,2,1,0:T(8,128)(2,1)} %own.5) | copy-start | bytes 1179652
  6.6 88.4 %all-gather.2.cloned.1.call-start = ((), (), s32[]{:S(2)}) async-start(), calls=%async_computation | async-start | bytes 5640192 | tf_op jit(solution)/shard_map/all_gather | solution.py:448
  12.2 7.0 %collective-permute-start.1 = (bf16[2,192]{1,0:T(2,128)(2,1)S(1)}, bf16[2,192]{1,0:T(2,128)(2,1)S(1)}, u32[]{:S(2)}, u32[]{:S(2)}) collective-permute-start(bf16[2,192]{1,0:T(2,128)(2,1)S(1)} %pad_maximum_fusion.5), channel_id=1, source_target_pairs={{0,1},{1,0},{2,3},{3,2},{4,5},{5,4},{6,7},{7,6},{8,9},{9,8},{10,11... | collective-permute-start | bytes 2312 | tf_op jit(solution)/shard_map/ppermute | solution.py:423
  15.2 12.0 %collective-permute-start.2 = (bf16[2,2,192,256]{3,2,1,0:T(8,128)(2,1)S(1)}, bf16[2,2,192,256]{3,2,1,0:T(8,128)(2,1)S(1)}, u32[]{:S(2)}, u32[]{:S(2)}) collective-permute-start(bf16[2,2,192,256]{3,2,1,0:T(8,128)(2,1)S(1)} %copy-done.4), channel_id=1, source_target_pairs={{0,1},{1,0},{2,3},{3,2},{4,5},{5,4},{6,7},{7,6},{8,9},{9,8},{10,11... | collective-permute-start | bytes 1179656 | tf_op jit(solution)/shard_map/ppermute | solution.py:423
  15.3 17.8 %collective-permute-start = (bf16[2,192,256]{2,1,0:T(8,128)(2,1)S(1)}, bf16[2,192,256]{2,1,0:T(8,128)(2,1)S(1)}, u32[]{:S(2)}, u32[]{:S(2)}) collective-permute-start(bf16[2,192,256]{2,1,0:T(8,128)(2,1)S(1)} %copy-done.1), channel_id=1, source_target_pairs={{0,1},{1,0},{2,3},{3,2},{4,5},{5,4},{6,7},{7,6},{8,9},{9,8},{10,11... | collective-permute-start | bytes 589832 | tf_op jit(solution)/shard_map/ppermute | solution.py:423
  17.3 36.2 %collective-permute-start.6 = (bf16[2,2,192,256]{3,2,1,0:T(8,128)(2,1)S(1)}, bf16[2,2,192,256]{3,2,1,0:T(8,128)(2,1)S(1)}, u32[]{:S(2)}, u32[]{:S(2)}) collective-permute-start(bf16[2,2,192,256]{3,2,1,0:T(8,128)(2,1)S(1)} %copy-done.5), channel_id=1, source_target_pairs={{0,1},{1,0},{2,3},{3,2},{4,5},{5,4},{6,7},{7,6},{8,9},{9,8},{10,11... | collective-permute-start | bytes 1179656 | tf_op jit(solution)/shard_map/ppermute | solution.py:423
  39.1 8.1 %collective-permute-start.3 = (bf16[192,256]{1,0:T(8,128)(2,1)S(1)}, bf16[192,256]{1,0:T(8,128)(2,1)S(1)}, u32[]{:S(2)}, u32[]{:S(2)}) collective-permute-start(bf16[192,256]{1,0:T(8,128)(2,1)S(1)} %get-tuple-element.25), channel_id=1, source_target_pairs={{0,2},{2,4},{4,6},{6,8},{8,10},{10,12},{12,14},{1,3},{3,5},{5,7},{... | collective-permute-start | bytes 294920 | tf_op jit(solution)/shard_map/ppermute | solution.py:426
  42.5 8.7 %collective-permute-start.4 = (bf16[192,256]{1,0:T(8,128)(2,1)S(1)}, bf16[192,256]{1,0:T(8,128)(2,1)S(1)}, u32[]{:S(2)}, u32[]{:S(2)}) collective-permute-start(bf16[192,256]{1,0:T(8,128)(2,1)S(1)} %get-tuple-element.26), channel_id=1, source_target_pairs={{2,0},{4,2},{6,4},{8,6},{10,8},{12,10},{14,12},{3,1},{5,3},{7,5},{... | collective-permute-start | bytes 294920 | tf_op jit(solution)/shard_map/ppermute | solution.py:429
  43.9 39.6 %collective-permute-start.12 = (bf16[2,2,4,192,128]{4,3,2,1,0:T(8,128)(2,1)S(1)}, bf16[2,2,4,192,128]{4,3,2,1,0:T(8,128)(2,1)S(1)}, u32[]{:S(2)}, u32[]{:S(2)}) collective-permute-start(bf16[2,2,4,192,128]{4,3,2,1,0:T(8,128)(2,1)S(1)} %pad_maximum_fusion), channel_id=1, source_target_pairs={{0,1},{1,0},{2,3},{3,2},{4,5},{5,4},{6,7},{7,6},{8,9},{9,8},{10,11... | collective-permute-start | bytes 2359304 | tf_op jit(solution)/shard_map/ppermute | solution.py:423
  52.3 12.3 %copy-start = (bf16[2,192,256]{2,1,0:T(8,128)(2,1)}, bf16[2,192,256]{2,1,0:T(8,128)(2,1)S(1)}, u32[]{:S(2)}) copy-start(bf16[2,192,256]{2,1,0:T(8,128)(2,1)S(1)} %add_convert_fusion.1.own) | copy-start | bytes 589828
  52.3 12.3 %collective-permute-start.5 = (bf16[2,192,256]{2,1,0:T(8,128)(2,1)S(1)}, bf16[2,192,256]{2,1,0:T(8,128)(2,1)S(1)}, u32[]{:S(2)}, u32[]{:S(2)}) collective-permute-start(bf16[2,192,256]{2,1,0:T(8,128)(2,1)S(1)} %add_convert_fusion.1.own), channel_id=1, source_target_pairs={{0,1},{1,0},{2,3},{3,2},{4,5},{5,4},{6,7},{7,6},{8,9},{9,8},{10,11... | collective-permute-start | bytes 589832 | tf_op jit(solution)/shard_map/ppermute | solution.py:423
  53.5 0.7 copy-start.6
  59.4 22.4 %copy-start.2 = (bf16[2,192,256]{2,1,0:T(8,128)(2,1)S(1)}, bf16[2,192,256]{2,1,0:T(8,128)(2,1)}, u32[]{:S(2)}) copy-start(bf16[2,192,256]{2,1,0:T(8,128)(2,1)} %own.4) | copy-start | bytes 589828
  70.5 7.3 %collective-permute-start.7 = (bf16[192,256]{1,0:T(8,128)(2,1)S(1)}, bf16[192,256]{1,0:T(8,128)(2,1)S(1)}, u32[]{:S(2)}, u32[]{:S(2)}) collective-permute-start(bf16[192,256]{1,0:T(8,128)(2,1)S(1)} %get-tuple-element.23), channel_id=1, source_target_pairs={{0,2},{2,4},{4,6},{6,8},{8,10},{10,12},{12,14},{1,3},{3,5},{5,7},{... | collective-permute-start | bytes 294920 | tf_op jit(solution)/shard_map/ppermute | solution.py:426
  74.7 7.0 %collective-permute-start.8 = (bf16[192,256]{1,0:T(8,128)(2,1)S(1)}, bf16[192,256]{1,0:T(8,128)(2,1)S(1)}, u32[]{:S(2)}, u32[]{:S(2)}) collective-permute-start(bf16[192,256]{1,0:T(8,128)(2,1)S(1)} %get-tuple-element.24), channel_id=1, source_target_pairs={{2,0},{4,2},{6,4},{8,6},{10,8},{12,10},{14,12},{3,1},{5,3},{7,5},{... | collective-permute-start | bytes 294920 | tf_op jit(solution)/shard_map/ppermute | solution.py:429
  82.8 23.1 %copy-start.3 = (bf16[2,192,256]{2,1,0:T(8,128)(2,1)}, bf16[2,192,256]{2,1,0:T(8,128)(2,1)S(1)}, u32[]{:S(2)}) copy-start(bf16[2,192,256]{2,1,0:T(8,128)(2,1)S(1)} %add_convert_fusion.own) | copy-start | bytes 589828
  82.8 5.7 %collective-permute-start.9 = (bf16[2,192,256]{2,1,0:T(8,128)(2,1)S(1)}, bf16[2,192,256]{2,1,0:T(8,128)(2,1)S(1)}, u32[]{:S(2)}, u32[]{:S(2)}) collective-permute-start(bf16[2,192,256]{2,1,0:T(8,128)(2,1)S(1)} %add_convert_fusion.own), channel_id=1, source_target_pairs={{0,1},{1,0},{2,3},{3,2},{4,5},{5,4},{6,7},{7,6},{8,9},{9,8},{10,11... | collective-permute-start | bytes 589832 | tf_op jit(solution)/shard_map/ppermute | solution.py:423
  88.6 17.3 %copy-start.10 = (bf16[2,192,256]{2,1,0:T(8,128)(2,1)}, bf16[2,192,256]{2,1,0:T(8,128)(2,1)S(1)}, u32[]{:S(2)}) copy-start(bf16[2,192,256]{2,1,0:T(8,128)(2,1)S(1)} %collective-permute-done.9.other) | copy-start | bytes 589828
  88.7 24.8 %collective-permute-start.10 = (bf16[2,384,256]{2,1,0:T(8,128)(2,1)S(1)}, bf16[2,384,256]{2,1,0:T(8,128)(2,1)S(1)}, u32[]{:S(2)}, u32[]{:S(2)}) collective-permute-start(bf16[2,384,256]{2,1,0:T(8,128)(2,1)S(1)} %maximum_select_fusion), channel_id=1, source_target_pairs={{0,2},{2,4},{4,6},{6,8},{8,10},{10,12},{12,14},{1,3},{3,5},{5,7},{... | collective-permute-start | bytes 1179656 | tf_op jit(solution)/shard_map/ppermute | solution.py:426
  93.6 19.9 %collective-permute-start.11 = (bf16[2,384,256]{2,1,0:T(8,128)(2,1)S(1)}, bf16[2,384,256]{2,1,0:T(8,128)(2,1)S(1)}, u32[]{:S(2)}, u32[]{:S(2)}) collective-permute-start(bf16[2,384,256]{2,1,0:T(8,128)(2,1)S(1)} %maximum_select_fusion), channel_id=1, source_target_pairs={{2,0},{4,2},{6,4},{8,6},{10,8},{12,10},{14,12},{3,1},{5,3},{7,5},{... | collective-permute-start | bytes 1179656 | tf_op jit(solution)/shard_map/ppermute | solution.py:429
  94.9 17.0 %copy-start.17 = (bf16[192]{0:T(256)(128)(2,1)S(1)}, bf16[192]{0:T(256)(128)(2,1)}, u32[]{:S(2)}) copy-start(bf16[192]{0:T(256)(128)(2,1)} %param.22) | copy-start | bytes 1156
  94.9 17.8 %copy-start.18 = (bf16[192]{0:T(256)(128)(2,1)S(1)}, bf16[192]{0:T(256)(128)(2,1)}, u32[]{:S(2)}) copy-start(bf16[192]{0:T(256)(128)(2,1)} %param.23) | copy-start | bytes 1156
  105.9 14.9 %collective-permute-start.13 = (bf16[8,192,128]{2,1,0:T(8,128)(2,1)}, bf16[8,192,128]{2,1,0:T(8,128)(2,1)S(1)}, u32[]{:S(2)}, u32[]{:S(2)}) collective-permute-start(bf16[8,192,128]{2,1,0:T(8,128)(2,1)} %get-tuple-element.19), channel_id=1, source_target_pairs={{0,2},{2,4},{4,6},{6,8},{8,10},{10,12},{12,14},{1,3},{3,5},{5,7},{... | collective-permute-start | bytes 1179656 | tf_op jit(solution)/shard_map/ppermute | solution.py:426
  110.5 10.3 %collective-permute-start.14 = (bf16[8,192,128]{2,1,0:T(8,128)(2,1)}, bf16[8,192,128]{2,1,0:T(8,128)(2,1)S(1)}, u32[]{:S(2)}, u32[]{:S(2)}) collective-permute-start(bf16[8,192,128]{2,1,0:T(8,128)(2,1)} %get-tuple-element.20), channel_id=1, source_target_pairs={{2,0},{4,2},{6,4},{8,6},{10,8},{12,10},{14,12},{3,1},{5,3},{7,5},{... | collective-permute-start | bytes 1179656 | tf_op jit(solution)/shard_map/ppermute | solution.py:429
  113.5 7.3 %copy-start.11 = (bf16[2,384,256]{2,1,0:T(8,128)(2,1)}, bf16[2,384,256]{2,1,0:T(8,128)(2,1)S(1)}, u32[]{:S(2)}) copy-start(bf16[2,384,256]{2,1,0:T(8,128)(2,1)S(1)} %collective-permute-done.10.above) | copy-start | bytes 1179652
  113.5 7.3 %copy-start.12 = (bf16[2,384,256]{2,1,0:T(8,128)(2,1)}, bf16[2,384,256]{2,1,0:T(8,128)(2,1)S(1)}, u32[]{:S(2)}) copy-start(bf16[2,384,256]{2,1,0:T(8,128)(2,1)S(1)} %collective-permute-done.11.below) | copy-start | bytes 1179652
  120.8 0.8 copy-start.13
  120.8 0.9 copy-start.14
  (3 other events, 2.1 us)
Sparse Core Ops, SparseCore 0:
  12.2 61.1 all-gather.1
where the time goes:
time: 152 us
  Pallas kernels  53 us (35%)
  waiting for transfers between devices  35.7 us (23%)
  starting transfers between devices  29.3 us (19%)
  local copies, waits for them, and re-layouts  15.5 us (10%)
  between operations  13.7 us (9%)
  other arithmetic  4.47 us (3%)
    pallas_call x6, Pallas kernels, call(): pl.pallas_call(body, name=name, grid=grid, in_specs=specs, out_specs=[in_...  53 us
    ppermute x4, starting transfers between devices, downward(): lax.ppermute(value, 'rows', [(i, i + 1) for i in range(row_count - 1)])  17.1 us
    ppermute x7, waiting for transfers between devices, other_half(): return lax.ppermute(value, 'chan', swap)  16.2 us
    ppermute x4, waiting for transfers between devices, downward(): lax.ppermute(value, 'rows', [(i, i + 1) for i in range(row_count - 1)])  11.4 us
    ppermute x4, waiting for transfers between devices, upward(): lax.ppermute(value, 'rows', [(i + 1, i) for i in range(row_count - 1)])  8.04 us
    ppermute x7, starting transfers between devices, other_half(): return lax.ppermute(value, 'chan', swap)  6.82 us
    ppermute x4, starting transfers between devices, upward(): lax.ppermute(value, 'rows', [(i + 1, i) for i in range(row_count - 1)])  5.35 us
    unnamed x39, local copies, waits for them, and re-layouts  3.82 us
  transfers between devices with their start and end apart: 16, of which 8 were waited for; matrix products, arithmetic and copies ran while one was open for 7% of the time, Pallas kernels for 20%

commit v1 on v0

v1 whole, which is shorter than its diff:
```python
import functools

import jax
import jax.numpy as jnp
from jax import lax
from jax.experimental import pallas as pl
from jax.experimental.pallas import tpu as pltpu
from jax.sharding import PartitionSpec as P

F32, BF16 = jnp.float32, jnp.bfloat16
MIB = 1024 * 1024


def in_vmem(*shape):
    return pl.BlockSpec(memory_space=pltpu.VMEM)


SCALAR = pl.BlockSpec(memory_space=pltpu.SMEM)


def size_of(shaped):
    rows = -(-shaped.shape[-2] // 16) * 16
    lanes = -(-shaped.shape[-1] // 128) * 128
    lead = 1
    for extent in shaped.shape[:-2]:
        lead *= extent
    return lead * rows * lanes * jnp.dtype(shaped.dtype).itemsize


def call(body, name, args, outs, scratch, flops):
    moved = sum(size_of(a) for a in args[1:]) + sum(size_of(o) for o in outs)
    held = moved + sum(size_of(jax.ShapeDtypeStruct(s.shape, s.dtype)) for s in scratch)
    return pl.pallas_call(
        body,
        name=name,
        in_specs=[SCALAR] + [in_vmem()] * (len(args) - 1),
        out_specs=[in_vmem()] * len(outs),
        out_shape=outs,
        scratch_shapes=scratch,
        compiler_params=pltpu.CompilerParams(vmem_limit_bytes=held + 4 * MIB),
        cost_estimate=pl.CostEstimate(flops=flops, bytes_accessed=moved, transcendentals=0),
    )(*args)


def silu_of(values, scale, gain):
    scaled = values * scale * gain
    return scaled / (1.0 + jnp.exp(-scaled))


def activated(values, gain):
    mean = jnp.mean(values * values, axis=0, keepdims=True)
    return silu_of(values, lax.rsqrt(mean + 1e-06), gain)


def column_of(gains, row):
    count = gains.shape[1]
    same = lax.broadcasted_iota(jnp.int32, (count, count), 0) == lax.broadcasted_iota(
        jnp.int32, (count, count), 1
    )
    turned = lax.dot_general(
        jnp.where(same, 1.0, 0.0).astype(BF16),
        gains,
        (((1,), (1,)), ((), ())),
        preferred_element_type=F32,
    )
    return turned[:, row : row + 1]


def rolled(value, step):
    count = value.shape[1]
    return value if step == 0 else pltpu.roll(value, step % count, 1)


def in_order(c, own, other):
    return jnp.where(c == 0, own, other), jnp.where(c == 0, other, own)


def spread(columns, base, stride, value, width, edged):
    depth, count = value.shape
    lane = lax.broadcasted_iota(jnp.int32, value.shape, 1)
    for j in range(3):
        moved = rolled(value, 1 - j)
        if edged and j == 0:
            moved = jnp.where(lane == 0, 0.0, moved)
        if edged and j == 2:
            moved = jnp.where(lane == count - 1, 0.0, moved)
        at = base + j * stride
        columns[at : at + depth, :] = moved[:, :width].astype(BF16)


def in_turn(count, fill, use, buffers):
    fill(0, buffers[0])

    def pair(k, _):
        for side in range(2):
            step = 2 * k + side
            fill(jnp.minimum(step + 1, count - 1), buffers[1 - side])
            use(step, buffers[side])
        return 0

    lax.fori_loop(0, count // 2, pair, 0)
    if count % 2:
        use(count - 1, buffers[0])


def low_sums(total, r, weights, first, frames, columns):
    outs, depth = weights.shape[3:]
    for i in range(3):
        sums = None
        for t in range(frames):
            left = jnp.concatenate([weights[first + t, i, j] for j in range(3)], axis=1)
            part = jnp.dot(
                left, columns[t * 3 * depth : (t + 1) * 3 * depth, :], preferred_element_type=F32
            )
            sums = part if sums is None else sums + part
        total[r + 2 - i] += sums


def low_cached_body(place, own, other, weights, total, *buffers):
    frames, rows, half, width = own.shape
    depth = 2 * half
    c = place[0]
    total[...] = jnp.zeros_like(total)

    def fill(r, columns):
        for t in range(frames):
            for at, value in enumerate(in_order(c, own[t, r], other[t, r])):
                base = t * 3 * depth + at * half
                spread(columns, base, depth, value.astype(F32), width, True)

    def use(r, columns):
        low_sums(total, r, weights, 0, frames, columns)

    in_turn(rows, fill, use, buffers)


def low_living_body(
    which, place, own, other, gain, other_gain, cached, weights, inner, red, black, total, *buffers
):
    rows, half, width = own.shape
    depth = 2 * half
    c, even = place[0], place[3]
    total[...] = cached[...]
    mine = column_of(gain[...], which)
    theirs = column_of(other_gain[...], which)

    def fill(r, columns):
        a, b = own[r].astype(F32), other[r].astype(F32)
        squares = jnp.sum(a * a, axis=0, keepdims=True) + jnp.sum(b * b, axis=0, keepdims=True)
        scale = lax.rsqrt(squares / depth + 1e-06)
        a, b = in_order(c, silu_of(a, scale, mine), silu_of(b, scale, theirs))
        spread(columns, 0, depth, a, width, True)
        spread(columns, half, depth, b, width, True)

    def use(r, columns):
        low_sums(total, r, weights, weights.shape[0] - 1, 1, columns)

    in_turn(rows, fill, use, buffers)
    inner[...] = total[1 : rows + 1]
    up, down = total[0].astype(BF16), total[rows + 1].astype(BF16)
    red[...] = jnp.where(even == 1, down, up)
    black[...] = jnp.where(even == 1, up, down)


def low_cached(place, own, other, kernel):
    frames, rows, half, width = own.shape
    outs, depth = kernel.shape[3:]
    return call(
        low_cached_body,
        "low_cached",
        (place, own, other, kernel),
        [jax.ShapeDtypeStruct((rows + 2, outs, width), F32)],
        [pltpu.VMEM((frames * 3 * depth, width), BF16)] * 2,
        2 * frames * 9 * outs * depth * rows * width,
    )[0]


def low_living(place, own, other, gain, other_gain, which, cached, kernel):
    rows, half, width = own.shape
    outs, depth = kernel.shape[3:]
    return call(
        functools.partial(low_living_body, which),
        "low_living",
        (place, own, other, gain, other_gain, cached, kernel),
        [
            jax.ShapeDtypeStruct((rows, outs, width), F32),
            jax.ShapeDtypeStruct((outs, width), BF16),
            jax.ShapeDtypeStruct((outs, width), BF16),
        ],
        [pltpu.VMEM((rows + 2, outs, width), F32)]
        + [pltpu.VMEM((3 * depth, width), BF16)] * 2,
        2 * 9 * outs * depth * rows * width,
    )


def one_hot(condition):
    return jnp.where(condition, 1.0, 0.0).astype(BF16)


def edge_body(place, cache_a, cache_b, packet):
    frames, rows, depth, width = cache_a.shape
    c = place[0]
    source = lax.broadcasted_iota(jnp.int32, (width, 128), 0)
    lane = lax.broadcasted_iota(jnp.int32, (width, 128), 1)
    start = jnp.where(c == 0, width - 2, 0)
    near = jnp.where(c == 0, width - 1, 0)
    sums = jnp.zeros((depth, 128), F32)
    for t in range(frames):
        for r in range(rows):
            k = lane - 2 * (t * rows + r)
            pick = one_hot((k >= 0) & (k < 2) & (source == start + k))
            sums += jnp.dot(cache_a[t, r], pick, preferred_element_type=F32)
            at = 2 * frames * rows + t * rows + r
            pick = one_hot((lane == at) & (source == near))
            sums += jnp.dot(cache_b[t, r], pick, preferred_element_type=F32)
    packet[...] = sums.astype(BF16)


def edges_of(place, cache_a, cache_b):
    frames, rows, depth, _ = cache_a.shape
    return call(
        edge_body,
        "edges",
        (place, cache_a, cache_b),
        [jax.ShapeDtypeStruct((depth, 128), BF16)],
        [],
        4 * frames * rows * depth * 256 * 128,
    )[0]


def close_body(place, latent, inner, red, black, kept, kept_edge, sent):
    rows, outs, width = latent.shape
    span = width // 2
    c, even = place[0], place[3]
    source = lax.broadcasted_iota(jnp.int32, (width, 128), 0)
    lane = lax.broadcasted_iota(jnp.int32, (width, 128), 1)
    mine = jnp.where(c == 0, span, span - 2)
    theirs = jnp.where(c == 0, span - 2, span)
    edge_mine = jnp.zeros((outs, 128), F32)
    edge_theirs = jnp.zeros((outs, 128), F32)
    for r in range(rows):
        value = latent[r].astype(F32) + inner[r]
        if r == 0:
            value += jnp.where(even == 1, black[...], red[...]).astype(F32)
        if r == rows - 1:
            value += jnp.where(even == 1, red[...], black[...]).astype(F32)
        value = value.astype(BF16)
        left, right = value[:, :span], value[:, span:]
        kept[r] = jnp.where(c == 0, left, right)
        sent[r] = jnp.where(c == 0, right, left)
        k = lane - 2 * (c * rows + r)
        inside = (k >= 0) & (k < 2)
        edge_mine += jnp.dot(
            value, one_hot(inside & (source == mine + k)), preferred_element_type=F32
        )
        edge_theirs += jnp.dot(
            value, one_hot(inside & (source == theirs + k)), preferred_element_type=F32
        )
    kept_edge[...] = edge_mine.astype(BF16)
    sent[rows] = edge_theirs.astype(BF16)


def close(place, latent, inner, red, black):
    rows, outs, width = latent.shape
    span = width // 2
    return call(
        close_body,
        "close",
        (place, latent, inner, red, black),
        [
            jax.ShapeDtypeStruct((rows, outs, span), BF16),
            jax.ShapeDtypeStruct((outs, 128), BF16),
            jax.ShapeDtypeStruct((rows + 1, outs, span), BF16),
        ],
        [],
        4 * rows * outs * width * 128,
    )


def high_sums(total, first, weights, lanes, columns, width, share):
    outs = total.shape[1]
    group = min(2, outs // share)
    for s in range(0, outs // share, group):
        rows = slice(3 * s * share, 3 * (s + group) * share)
        part = jnp.dot(
            left_of(weights, 3 * outs, rows, *lanes), columns[:, :width], preferred_element_type=F32
        )
        for g in range(group):
            for i in range(3):
                at = 3 * g + i
                total[first + 2 - i, (s + g) * share : (s + g + 1) * share, :] += part[
                    at * share : (at + 1) * share
                ]


def left_of(weights, height, rows, first, last):
    lanes = weights.shape[1]
    parts = []
    while first < last:
        piece, start = divmod(first, lanes)
        stop = min(lanes, start + last - first)
        parts.append(weights[piece * height + rows.start : piece * height + rows.stop, start:stop])
        first += stop - start
    return parts[0] if len(parts) == 1 else jnp.concatenate(parts, axis=1)


def kept_lanes(c, width, shape):
    lane = lax.broadcasted_iota(jnp.int32, shape, 1)
    count = shape[1]
    middle = (width + count) // 2
    return (lane < jnp.where(c == 0, middle, width)) | (lane >= jnp.where(c == 0, count, middle))


def high_cached_body(
    share, place, own_a, own_b, edge, weights, sums_a, sums_b, red, black, total_a, total_b,
    columns_a0, columns_a1, columns_b0, columns_b1,
):
    frames, rows, depth, width = own_a.shape
    count = total_a.shape[2]
    c, even = place[0], place[3]
    total_a[...] = jnp.zeros_like(total_a)
    total_b[...] = jnp.zeros_like(total_b)
    long = frames * 3 * depth
    second = long + 6 * depth
    lane = lax.broadcasted_iota(jnp.int32, (depth, 128), 1)

    def fill(r, columns):
        for t in range(frames):
            at = t * rows + r
            first = jnp.where(c == 0, 0, 126)
            moved = pltpu.roll(edge[...].astype(F32), (first - 2 * at + 256) % 128, 1)
            beside = jnp.where((lane >= first) & (lane < first + 2), moved, 0.0)
            value = jnp.concatenate([own_a[t, r].astype(F32), beside], axis=1)
            spread(columns[0], t * 3 * depth, depth, value, count, False)
            at += 2 * frames * rows
            first = jnp.where(c == 0, 0, 127)
            moved = pltpu.roll(edge[...].astype(F32), (first - at + 256) % 128, 1)
            beside = jnp.where(lane == first, moved, 0.0)
            value = jnp.concatenate([own_b[t, r].astype(F32), beside], axis=1)
            spread(columns[1], t * 3 * depth, depth, value, width, False)

    def use(r, columns):
        high_sums(total_a, r, weights, (0, long), columns[0], count, share)
        high_sums(total_b, r, weights, (second, second + long), columns[1], width, share)

    in_turn(rows, fill, use, ((columns_a0, columns_b0), (columns_a1, columns_b1)))
    sums_a[...] = total_a[...]
    sums_b[...] = total_b[1 : rows + 1]
    spot = 0
    for source, top, bottom in (
        (total_a, 0, rows), (total_a, 1, rows + 1), (total_b, 0, rows + 1)
    ):
        for start in range(0, source.shape[2], 128):
            lanes = slice(start, start + 128)
            up, down = source[top, :, lanes].astype(BF16), source[bottom, :, lanes].astype(BF16)
            red[spot] = jnp.where(even == 1, down, up)
            black[spot] = jnp.where(even == 1, up, down)
            spot += 1


def high_cached(place, own_a, own_b, edge, weights, share):
    frames, rows, depth, width = own_a.shape
    count = width + 128
    blocks = (2 * count + width) // 128
    return call(
        functools.partial(high_cached_body, share),
        "high_cached",
        (place, own_a, own_b, edge, weights),
        [
            jax.ShapeDtypeStruct((rows + 2, depth, count), F32),
            jax.ShapeDtypeStruct((rows, depth, width), F32),
            jax.ShapeDtypeStruct((blocks, depth, 128), BF16),
            jax.ShapeDtypeStruct((blocks, depth, 128), BF16),
        ],
        [
            pltpu.VMEM((rows + 2, depth, count), F32),
            pltpu.VMEM((rows + 2, depth, width), F32),
        ]
        + [pltpu.VMEM((frames * 3 * depth, count), BF16)] * 2
        + [pltpu.VMEM((frames * 3 * depth, width), BF16)] * 2,
        2 * frames * 9 * depth * depth * rows * (width + count),
    )


def high_living_body(
    share, place, one, above, below, gain_a, gain_b, sums_a, sums_b, red, black, weights, decoded,
    wide, total, total_a, total_b, resampled, columns_r0, columns_r1, columns_0, columns_1,
):
    blocks, half, span = one.shape
    rows = (blocks - 1) // 2
    high_rows, outs, width = decoded.shape
    count = sums_a.shape[2]
    c, first, last, even = place[0], place[1], place[2], place[3]
    depth = 2 * half
    long = 6 * outs
    keep = kept_lanes(c, width, (outs, count))

    lane = lax.broadcasted_iota(jnp.int32, (span + 128, count), 1)
    source = lax.broadcasted_iota(jnp.int32, (span + 128, count), 0)
    column = jnp.where((c == 1) & (lane >= (width + count) // 2), lane - count, lane) + c * width
    low = column >> 1
    inside = low - c * span
    k = low - jnp.where(c == 0, span, span - 2)
    own_lane = (source == inside) & (inside < span)
    for g in range(2):
        for r in range(rows):
            edge_lane = (source == span + 2 * (g * rows + r) + k) & (k >= 0) & (k < 2)
            edge_lane = edge_lane & ((inside < 0) | (inside >= span))
            spot = kept_lanes(c, width, column.shape) & (own_lane | edge_lane)
            wide[g * rows + r] = one_hot(spot)

    total[...] = jnp.zeros_like(total)

    def fill_low(tile, r, columns):
        for at, value in enumerate(in_order(c, tile[r], tile[rows + r])):
            value = jnp.concatenate([value, tile[2 * rows]], axis=1)
            value = jnp.dot(value, wide[at * rows + r], preferred_element_type=F32)
            spread(columns, at * half, depth, value, count, False)

    def use_low(m, columns):
        group = min(2, outs // share)
        for s in range(0, outs // share, group):
            picked = slice(3 * s * share, 3 * (s + group) * share)
            part = jnp.dot(
                left_of(weights, 3 * outs, picked, 3 * long, 3 * long + 3 * depth),
                columns[...],
                preferred_element_type=F32,
            )
            for g in range(group):
                at = slice((s + g) * share, (s + g + 1) * share)
                p0, p1, p2 = (
                    part[(3 * g + i) * share : (3 * g + i + 1) * share] for i in range(3)
                )
                total[2 * m, at, :] += p2
                total[2 * m + 1, at, :] += p1 + p2
                total[2 * m + 2, at, :] += p0 + p1
                total[2 * m + 3, at, :] += p0

    buffers = (columns_r0, columns_r1)
    steps = [(one, rows)] + [(above, 0)] + [(below, 2 * rows)]
    steps = [(tile, r, at + r) for tile, at in steps for r in range(rows)]
    fill_low(steps[0][0], steps[0][1], buffers[0])
    for k, (tile, r, at) in enumerate(steps):
        if k + 1 < len(steps):
            fill_low(steps[k + 1][0], steps[k + 1][1], buffers[(k + 1) % 2])
        use_low(at, buffers[k % 2])

    spare = 2 * rows - 1
    total_a[...] = jnp.zeros_like(total_a)
    total_a[2 : high_rows + 4] = sums_a[...]
    total_b[...] = jnp.zeros_like(total_b)
    total_b[2 : high_rows + 2] = sums_b[...]
    spot = 0
    for target, top, bottom in (
        (total_a, 2, high_rows + 2), (total_a, 3, high_rows + 3), (total_b, 2, high_rows + 1)
    ):
        for start in range(0, target.shape[2], 128):
            lanes = slice(start, start + 128)
            a, b = red[spot].astype(F32), black[spot].astype(F32)
            target[top, :, lanes] += jnp.where(even == 1, b, a)
            target[bottom, :, lanes] += jnp.where(even == 1, a, b)
            spot += 1

    buffers = (columns_0, columns_1)
    pad = columns_0.shape[0] - 3 * outs
    for columns in buffers:
        columns[3 * outs :, :] = jnp.zeros((pad, count), BF16)
    left_a, left_b = column_of(gain_a[...], 0), column_of(gain_b[...], 0)

    def fill_a(h, columns):
        outside = ((first == 1) & (h < 2)) | ((last == 1) & (h >= high_rows + 2))
        value = jnp.where(keep, total[h + spare], 0.0).astype(BF16)
        value = jnp.where(outside, jnp.zeros_like(value), value)
        resampled[h] = value
        spread(columns, 0, outs, activated(value.astype(F32), left_a), count, False)

    def use_a(h, columns):
        high_sums(
            total_a, h, weights, (long, long + columns.shape[0]), columns, count, share
        )

    in_turn(high_rows + 4, fill_a, use_a, buffers)
    for columns in buffers:
        columns[:pad, :] = jnp.zeros((pad, count), BF16)

    def fill_b(h, columns):
        outside = ((first == 1) & (h < 1)) | ((last == 1) & (h >= high_rows + 1))
        value = jnp.where(keep, total_a[h + 2], 0.0).astype(BF16)
        value = jnp.where(outside, jnp.zeros_like(value), value)
        spread(columns, pad, outs, activated(value.astype(F32), left_b), count, False)

    def use_b(h, columns):
        high_sums(
            total_b, h, weights, (2 * long - columns.shape[0], 2 * long), columns, width, share
        )

    in_turn(high_rows + 2, fill_b, use_b, buffers)
    for h in range(high_rows):
        decoded[h] = (total_b[h + 2] + resampled[h + 2, :, :width].astype(F32)).astype(BF16)


def high_living(
    place, one, above, below, gain_a, gain_b, sums_a, sums_b, red, black, weights, share
):
    blocks, half, span = one.shape
    rows = (blocks - 1) // 2
    high_rows, outs, width = sums_b.shape
    count = sums_a.shape[2]
    depth = 2 * half
    padded = -(-3 * outs // 128) * 128
    return call(
        functools.partial(high_living_body, share),
        "high_living",
        (place, one, above, below, gain_a, gain_b, sums_a, sums_b, red, black, weights),
        [jax.ShapeDtypeStruct((high_rows, outs, width), BF16)],
        [
            pltpu.VMEM((2 * rows, span + 128, count), BF16),
            pltpu.VMEM((6 * rows + 2, outs, count), F32),
            pltpu.VMEM((high_rows + 6, outs, count), F32),
            pltpu.VMEM((high_rows + 4, outs, width), F32),
            pltpu.VMEM((high_rows + 4, outs, count), BF16),
        ]
        + [pltpu.VMEM((3 * depth, count), BF16)] * 2
        + [pltpu.VMEM((padded, count), BF16)] * 2,
        2 * 27 * outs * outs * high_rows * width + 2 * 9 * outs * depth * high_rows * count,
    )[0]


def body(
    latent,
    cache_low_a,
    cache_low_b,
    gain_low_a,
    gain_low_b,
    kernel_low_a,
    kernel_low_b,
    resample_kernel,
    gain_high_a,
    gain_high_b,
    kernel_high_a,
    kernel_high_b,
    cache_high_a,
    cache_high_b,
):
    c = lax.axis_index("chan")
    r = lax.axis_index("rows")
    row_count = lax.axis_size("rows")
    swap = [(0, 1), (1, 0)]

    def other_half(value):
        return lax.ppermute(value, "chan", swap)

    reds = [(i, i ^ 1) for i in range(row_count) if i ^ 1 < row_count]
    blacks = [(i, i + 1 if i % 2 else i - 1) for i in range(1, row_count - 1 + row_count % 2)]

    def by_red(value):
        return lax.ppermute(value, "rows", reds)

    def by_black(value):
        return lax.ppermute(value, "rows", blacks)

    even = r % 2 == 0
    place = jnp.stack([c, r == 0, r == row_count - 1, even]).astype(jnp.int32)

    share = kernel_high_a.shape[3]

    def flat(kernel):
        turned = jnp.transpose(kernel, (1, 3, 0, 2, 4))
        return turned.reshape(3 * share, -1)

    flat_a, flat_b = flat(kernel_high_a), flat(kernel_high_b)
    flat_r = flat(resample_kernel[None])
    outs = kernel_high_a.shape[4]
    long = 6 * outs
    lined = jnp.concatenate([flat_a, flat_b[:, long:], flat_b[:, :long], flat_r], axis=1)
    pieces = lax.axis_size("views")
    lanes = -(-lined.shape[1] // (128 * pieces)) * 128
    lined = jnp.pad(lined, ((0, 0), (0, lanes * pieces - lined.shape[1])))
    mine = lax.dynamic_slice_in_dim(lined, lax.axis_index("views") * lanes, lanes, 1)
    weights = lax.all_gather(mine, ("views", "rows"), axis=0, tiled=True)
    if share % 8:
        weights = weights.reshape(pieces, -1, 3, share, lanes).transpose(0, 2, 1, 3, 4)
        weights = weights.reshape(-1, lanes)
        share = outs

    rows, half, low_width = latent.shape
    gains = jnp.pad(jnp.stack([gain_low_a, gain_low_b]), ((0, 14), (0, 0)))
    sent = jnp.pad(gains, ((0, 0), (0, low_width - half)))
    sent = jnp.concatenate([latent.reshape(rows * half, low_width), sent])
    got = other_half(sent)
    other_latent = got[: rows * half].reshape(latent.shape)
    other_gains = got[rows * half :, :half]
    other_cache_a = other_half(cache_low_a)
    other_cache_b = other_half(cache_low_b)
    edge = other_half(edges_of(place, cache_high_a, cache_high_b))

    def low_conv(inputs, other, cached, which, kernel):
        inner, red, black = low_living(
            place, inputs, other, gains, other_gains, which, cached, kernel
        )
        return inner, by_red(red), by_black(black)

    cached_a = low_cached(place, cache_low_a, other_cache_a, kernel_low_a)
    cached_b = low_cached(place, cache_low_b, other_cache_b, kernel_low_b)
    inner, red, black = low_conv(latent, other_latent, cached_a, 0, kernel_low_a)
    top = jnp.where(even, black, red).astype(F32)
    bottom = jnp.where(even, red, black).astype(F32)
    middle_low = jnp.concatenate(
        [inner[:1] + top, inner[1:-1], inner[-1:] + bottom]
    ).astype(BF16)
    inner, red, black = low_conv(middle_low, other_half(middle_low), cached_b, 1, kernel_low_b)
    kept, kept_edge, sent = close(place, latent, inner, red, black)
    got = other_half(sent)
    one = jnp.concatenate([kept, got[:rows], (kept_edge + got[rows])[None]])
    from_red, from_black = by_red(one), by_black(one)
    above = jnp.where(even, from_black, from_red)
    below = jnp.where(even, from_red, from_black)

    sums_a, sums_b, red, black = high_cached(
        place, cache_high_a, cache_high_b, edge, weights, share
    )
    return high_living(
        place,
        one,
        above,
        below,
        jnp.pad(gain_high_a[None], ((0, 15), (0, 0))),
        jnp.pad(gain_high_b[None], ((0, 15), (0, 0))),
        sums_a,
        sums_b,
        by_red(red),
        by_black(black),
        weights,
        share,
    )


def solution(mesh):
    placed = (
        P(("views", "rows"), "chan", None),
        P(None, ("views", "rows"), "chan", None),
        P(None, ("views", "rows"), "chan", None),
        P("chan"),
        P("chan"),
        P(None, None, None, "chan", None),
        P(None, None, None, "chan", None),
        P(None, None, "rows", None),
        P(),
        P(),
        P(None, None, None, "rows", None),
        P(None, None, None, "rows", None),
        P(None, ("views", "rows"), None, "chan"),
        P(None, ("views", "rows"), None, "chan"),
    )
    return jax.shard_map(
        body,
        mesh=mesh,
        in_specs=placed,
        out_specs=P(("views", "rows"), None, "chan"),
        check_vma=False,
    )
```

time: 152 us -> 125 us (0.82)
  Pallas kernels: 53 us -> 33.9 us
  local copies, waits for them, and re-layouts: 15.5 us -> 10.1 us
  waiting for transfers between devices: 35.7 us -> 40.6 us
  other arithmetic: 4.47 us -> 0.26 us
  starting transfers between devices: 29.3 us -> 25.5 us
    pallas_call x6 -> x8, Pallas kernels: 53 us -> 33.9 us  [call(): pl.pallas_call(body, name=name, in_specs=[SCALAR] + [in_vmem()] * (len(ar...]
    ppermute x7 -> x6, waiting for transfers between devices: 16.2 us -> 23 us  [other_half(): return lax.ppermute(value, 'chan', swap)]
    ppermute x8, starting transfers between devices: 22.4 us -> 17 us  [the longest x4 14.2 us: by_red(): return lax.ppermute(value, 'rows', reds)]
    convert_element_type x4 -> x0, other arithmetic: 3.52 us -> none  [the longest x2 1.42 us: column_of(): return jnp.where(c == 0, jnp.concatenate([gain, other]), jnp.concatenate(...]
    squeeze x3 -> x0, local copies, waits for them, and re-layouts: 2.86 us -> none  [the longest x2 1.91 us: level1_conv(): from_above = downward(edges[1])]
    ppermute x8, waiting for transfers between devices: 19.4 us -> 17.2 us  [the longest x4 17.1 us: by_red(): return lax.ppermute(value, 'rows', reds)]
    ppermute x7 -> x6, starting transfers between devices: 6.82 us -> 8.4 us  [other_half(): return lax.ppermute(value, 'chan', swap)]
    unnamed x39 -> x29, local copies, waits for them, and re-layouts: 3.82 us -> 4.72 us
  transfers between devices with their start and end apart: 16 -> 15, of which waited for: 8 -> 7; matrix products, arithmetic and copies ran while one was open for 7% -> 0% of each run, Pallas kernels for 20% -> 14%
where the time goes in v1:
time: 125 us; the launch traced here: 124 us
  waiting for transfers between devices  40.6 us (32%)
  Pallas kernels  33.9 us (27%)
  starting transfers between devices  25.5 us (20%)
  between operations  13.8 us (11%)
  local copies, waits for them, and re-layouts  10.1 us (8%)
    pallas_call x8, Pallas kernels, call(): pl.pallas_call(body, name=name, in_specs=[SCALAR] + [in_vmem()] * (len(ar...  33.9 us
    ppermute x6, waiting for transfers between devices, other_half(): return lax.ppermute(value, 'chan', swap)  23 us
    ppermute x4, waiting for transfers between devices, by_red(): return lax.ppermute(value, 'rows', reds)  17.1 us
    ppermute x4, starting transfers between devices, by_red(): return lax.ppermute(value, 'rows', reds)  14.2 us
    ppermute x6, starting transfers between devices, other_half(): return lax.ppermute(value, 'chan', swap)  8.4 us
    unnamed x29, local copies, waits for them, and re-layouts  4.72 us
    transpose x3, local copies, waits for them, and re-layouts, flat(): turned = jnp.transpose(kernel, (1, 3, 0, 2, 4))  3.36 us
    ppermute x4, starting transfers between devices, by_black(): return lax.ppermute(value, 'rows', blacks)  2.84 us
  transfers between devices with their start and end apart: 15, of which 7 were waited for; matrix products, arithmetic and copies ran while one was open for 0% of the time, Pallas kernels for 14%

profile of v1, /device:TPU:0, one launch (start us, length us, event | category | flops | bytes accessed | tf_op | source)
XLA Modules:
  0.0 124.1 jit_solution(12376913482610567412)
XLA Ops:
  6.6 1.2 copy.19
  8.1 1.0 copy.20
  9.2 1.1 copy.18
  10.6 0.7 concatenate.16
  11.3 0.8 constant_dynamic-slice_fusion
  12.1 3.1 %collective-permute-start.1 = (bf16[2,2,192,256]{3,2,1,0:T(8,128)(2,1)S(1)}, bf16[2,2,192,256]{3,2,1,0:T(8,128)(2,1)S(1)}, u32[]{:S(2)}, u32[]{:S(2)}) collective-permute-start(bf16[2,2,192,256]{3,2,1,0:T(8,128)(2,1)S(1)} %copy-done.6), channel_id=1, source_target_pairs={{0,1},{1,0},{2,3},{3,2},{4,5},{5,4},{6,7},{7,6},{8,9},{9,8},{10,11... | collective-permute-start | bytes 1179656 | tf_op jit(solution)/shard_map/ppermute | solution.py:551
  15.4 13.3 %collective-permute-done = bf16[400,256]{1,0:T(8,128)(2,1)S(1)} collective-permute-done((bf16[400,256]{1,0:T(8,128)(2,1)S(1)}, bf16[400,256]{1,0:T(8,128)(2,1)S(1)}, u32[]{:S(2)}, u32[]{:S(2)}) %collective-permute-start) | collective-permute-done | bytes 204832 | tf_op jit(solution)/shard_map/ppermute | solution.py:551
  28.7 2.1 %copy-done = bf16[3,3,3,192,384]{4,3,2,1,0:T(8,128)(2,1)S(1)} copy-done((bf16[3,3,3,192,384]{4,3,2,1,0:T(8,128)(2,1)S(1)}, bf16[3,3,3,192,384]{4,3,2,1,0:T(8,128)(2,1)}, u32[]{:S(2)}) %copy-start) | copy-done | bytes 3981336
  30.8 2.4 %low_cached.2.cached = f32[4,192,256]{2,1,0:T(8,128)S(1)} custom-call(s32[4]{0:T(128)S(1)} %pad_add_fusion.place, bf16[2,2,192,256]{3,2,1,0:T(8,128)(2,1)S(1)} %copy-done.6, bf16[2,2,192,256]{3,2,1,0:T(8,128)(2,1)S(1)} %collective-permute-done.1.other, bf16[3,3,3,192,384]{4,3,2,1,0:T(8,128)(2,1)S(1)} %copy-done), custom_call_target="tpu_custom_call" | custom-call | flops 1358954496 | bytes 5554176 | tf_op jit(solution)/shard_map/low_cached/pallas_call | solution.py:33
  33.2 2.0 %low_living.2 = (f32[2,192,256]{2,1,0:T(8,128)S(1)}, bf16[192,256]{1,0:T(8,128)(2,1)S(1)}, bf16[192,256]{1,0:T(8,128)(2,1)S(1)}) custom-call(s32[4]{0:T(128)S(1)} %pad_add_fusion.place, bf16[2,192,256]{2,1,0:T(8,128)(2,1)S(1)} %copy-done.3, bf16[2,192,256]{2,1,0:T(8,128)(2,1)S(1)} %bitcast.30, bf16[16,192]{1,0:T(8,128)(2,1)S(1)} %fusion.8.gain, ...), custom_call_target="tpu_custom_call" | custom-call | flops 679477248 | bytes 5767168 | tf_op jit(solution)/shard_map/low_living/pallas_call | solution.py:33
  35.2 0.7 collective-permute-start.2
  35.9 4.6 %collective-permute-start.3 = (bf16[192,256]{1,0:T(8,128)(2,1)S(1)}, bf16[192,256]{1,0:T(8,128)(2,1)S(1)}, u32[]{:S(2)}, u32[]{:S(2)}) collective-permute-start(bf16[192,256]{1,0:T(8,128)(2,1)S(1)} %get-tuple-element.20), channel_id=1, source_target_pairs={{0,2},{2,0},{4,6},{6,4},{8,10},{10,8},{12,14},{14,12},{1,3},{3,1},... | collective-permute-start | bytes 294920 | tf_op jit(solution)/shard_map/ppermute | solution.py:557
  40.5 1.5 %collective-permute-start.5 = (bf16[2,2,192,256]{3,2,1,0:T(8,128)(2,1)S(1)}, bf16[2,2,192,256]{3,2,1,0:T(8,128)(2,1)S(1)}, u32[]{:S(2)}, u32[]{:S(2)}) collective-permute-start(bf16[2,2,192,256]{3,2,1,0:T(8,128)(2,1)S(1)} %copy-done.7), channel_id=1, source_target_pairs={{0,1},{1,0},{2,3},{3,2},{4,5},{5,4},{6,7},{7,6},{8,9},{9,8},{10,11... | collective-permute-start | bytes 1179656 | tf_op jit(solution)/shard_map/ppermute | solution.py:551
  42.0 1.2 collective-permute-done.3
  43.2 1.6 %collective-permute-start.4 = (bf16[2,192,256]{2,1,0:T(8,128)(2,1)S(1)}, bf16[2,192,256]{2,1,0:T(8,128)(2,1)S(1)}, u32[]{:S(2)}, u32[]{:S(2)}) collective-permute-start(bf16[2,192,256]{2,1,0:T(8,128)(2,1)S(1)} %pad_maximum_fusion.1.own), channel_id=1, source_target_pairs={{0,1},{1,0},{2,3},{3,2},{4,5},{5,4},{6,7},{7,6},{8,9},{9,8},{10,11... | collective-permute-start | bytes 589832 | tf_op jit(solution)/shard_map/ppermute | solution.py:551
  44.8 7.3 %collective-permute-done.5.other = bf16[2,2,192,256]{3,2,1,0:T(8,128)(2,1)S(1)} collective-permute-done((bf16[2,2,192,256]{3,2,1,0:T(8,128)(2,1)S(1)}, bf16[2,2,192,256]{3,2,1,0:T(8,128)(2,1)S(1)}, u32[]{:S(2)}, u32[]{:S(2)}) %collective-permute-start.5) | collective-permute-done | bytes 393248 | tf_op jit(solution)/shard_map/ppermute | solution.py:551
  52.1 2.4 %low_cached.3.cached = f32[4,192,256]{2,1,0:T(8,128)S(1)} custom-call(s32[4]{0:T(128)S(1)} %pad_add_fusion.place, bf16[2,2,192,256]{3,2,1,0:T(8,128)(2,1)S(1)} %copy-done.7, bf16[2,2,192,256]{3,2,1,0:T(8,128)(2,1)S(1)} %collective-permute-done.5.other, bf16[3,3,3,192,384]{4,3,2,1,0:T(8,128)(2,1)S(1)} %copy-done.2), custom_call_target="tpu_custom_call" | custom-call | flops 1358954496 | bytes 5554176 | tf_op jit(solution)/shard_map/low_cached/pallas_call | solution.py:33
  54.6 2.0 %low_living.3 = (f32[2,192,256]{2,1,0:T(8,128)S(1)}, bf16[192,256]{1,0:T(8,128)(2,1)S(1)}, bf16[192,256]{1,0:T(8,128)(2,1)S(1)}) custom-call(s32[4]{0:T(128)S(1)} %pad_add_fusion.place, bf16[2,192,256]{2,1,0:T(8,128)(2,1)S(1)} %pad_maximum_fusion.1.own, bf16[2,192,256]{2,1,0:T(8,128)(2,1)S(1)} %collective-permute-done.4.other, ...), custom_call_target="tpu_custom_call" | custom-call | flops 679477248 | bytes 5767168 | tf_op jit(solution)/shard_map/low_living/pallas_call | solution.py:33
  57.0 0.7 collective-permute-start.7
  57.7 3.9 %collective-permute-done.6.red = bf16[192,256]{1,0:T(8,128)(2,1)S(1)} collective-permute-done((bf16[192,256]{1,0:T(8,128)(2,1)S(1)}, bf16[192,256]{1,0:T(8,128)(2,1)S(1)}, u32[]{:S(2)}, u32[]{:S(2)}) %collective-permute-start.6) | collective-permute-done | bytes 98336 | tf_op jit(solution)/shard_map/ppermute | solution.py:557
  61.5 0.9 close.1
  62.4 1.5 %collective-permute-start.8 = (bf16[3,192,128]{2,1,0:T(8,128)(2,1)S(1)}, bf16[3,192,128]{2,1,0:T(8,128)(2,1)S(1)}, u32[]{:S(2)}, u32[]{:S(2)}) collective-permute-start(bf16[3,192,128]{2,1,0:T(8,128)(2,1)S(1)} %get-tuple-element.25), channel_id=1, source_target_pairs={{0,1},{1,0},{2,3},{3,2},{4,5},{5,4},{6,7},{7,6},{8,9},{9,8},{10,11... | collective-permute-start | bytes 442376 | tf_op jit(solution)/shard_map/ppermute | solution.py:551
  64.0 1.1 edges.1
  65.7 2.5 %collective-permute-done.8 = bf16[3,192,128]{2,1,0:T(8,128)(2,1)S(1)} collective-permute-done((bf16[3,192,128]{2,1,0:T(8,128)(2,1)S(1)}, bf16[3,192,128]{2,1,0:T(8,128)(2,1)S(1)}, u32[]{:S(2)}, u32[]{:S(2)}) %collective-permute-start.8) | collective-permute-done | bytes 147488 | tf_op jit(solution)/shard_map/ppermute | solution.py:551
  68.2 4.5 %collective-permute-start.10 = (bf16[5,192,128]{2,1,0:T(8,128)(2,1)S(1)}, bf16[5,192,128]{2,1,0:T(8,128)(2,1)S(1)}, u32[]{:S(2)}, u32[]{:S(2)}) collective-permute-start(bf16[5,192,128]{2,1,0:T(8,128)(2,1)S(1)} %pad_maximum_fusion.one), channel_id=1, source_target_pairs={{0,2},{2,0},{4,6},{6,4},{8,10},{10,8},{12,14},{14,12},{1,3},{3,1},... | collective-permute-start | bytes 737288 | tf_op jit(solution)/shard_map/ppermute | solution.py:557
  72.8 0.8 collective-permute-start.9
  74.0 2.5 %copy-done.8 = bf16[1152,2304]{1,0:T(8,128)(2,1)S(1)} copy-done((bf16[1152,2304]{1,0:T(8,128)(2,1)S(1)}, bf16[1152,2304]{1,0:T(8,128)(2,1)}, u32[]{:S(2)}) %copy-start.8) | copy-done | bytes 5308440
  76.5 6.8 %high_cached.1 = (f32[6,192,384]{2,1,0:T(8,128)S(1)}, f32[4,192,256]{2,1,0:T(8,128)S(1)}, bf16[8,192,128]{2,1,0:T(8,128)(2,1)S(1)}, bf16[8,192,128]{2,1,0:T(8,128)(2,1)S(1)}) custom-call(s32[4]{0:T(128)S(1)} %pad_add_fusion.place, bf16[2,4,192,256]{3,2,1,0:T(8,128)(2,1)S(1)} %copy-done.4, bf16[2,4,192,256]{3,2,1,0:T(8,128)(2,1)S(1)} %copy-done.5, ...), custom_call_target="tpu_custom_call" | custom-call | flops 3397386240 | bytes 10272768 | tf_op jit(solution)/shard_map/high_cached/pallas_call | solution.py:33
  83.4 4.7 %collective-permute-start.12 = (bf16[8,192,128]{2,1,0:T(8,128)(2,1)S(1)}, bf16[8,192,128]{2,1,0:T(8,128)(2,1)S(1)}, u32[]{:S(2)}, u32[]{:S(2)}) collective-permute-start(bf16[8,192,128]{2,1,0:T(8,128)(2,1)S(1)} %get-tuple-element.29), channel_id=1, source_target_pairs={{0,2},{2,0},{4,6},{6,4},{8,10},{10,8},{12,14},{14,12},{1,3},{3,1},... | collective-permute-start | bytes 1179656 | tf_op jit(solution)/shard_map/ppermute | solution.py:557
  88.1 0.7 collective-permute-start.13
  88.9 12.1 %collective-permute-done.12.red = bf16[8,192,128]{2,1,0:T(8,128)(2,1)S(1)} collective-permute-done((bf16[8,192,128]{2,1,0:T(8,128)(2,1)S(1)}, bf16[8,192,128]{2,1,0:T(8,128)(2,1)S(1)}, u32[]{:S(2)}, u32[]{:S(2)}) %collective-permute-start.12) | collective-permute-done | bytes 393248 | tf_op jit(solution)/shard_map/ppermute | solution.py:557
  101.0 16.3 %high_living.1 = bf16[4,192,256]{2,1,0:T(8,128)(2,1)} custom-call(s32[4]{0:T(128)S(1)} %pad_add_fusion.place, bf16[5,192,128]{2,1,0:T(8,128)(2,1)S(1)} %pad_maximum_fusion.one, bf16[5,192,128]{2,1,0:T(8,128)(2,1)S(1)} %get-tuple-element.34.above, bf16[5,192,128]{2,1,0:T(8,128)(2,1)S(1)} %get-tuple-element.33.below, bf16[16,192]{1,0:T(8,128)(2,1)S(1)} %pad.17.gain_a, ...), custom_call_target="tpu_custom_call" | custom-call | flops 4076863488 | bytes 9797632 | tf_op jit(solution)/shard_map/high_living/pallas_call | solution.py:33
  (62 shorter events, 2.6 us)
Async XLA Ops:
  6.5 5.5 %copy-start.6 = (bf16[2,2,192,256]{3,2,1,0:T(8,128)(2,1)S(1)}, bf16[2,2,192,256]{3,2,1,0:T(8,128)(2,1)}, u32[]{:S(2)}) copy-start(bf16[2,2,192,256]{3,2,1,0:T(8,128)(2,1)} %own.3) | copy-start | bytes 1179652
  6.5 8.6 %copy-start.10 = (bf16[192]{0:T(256)(128)(2,1)S(1)}, bf16[192]{0:T(256)(128)(2,1)}, u32[]{:S(2)}) copy-start(bf16[192]{0:T(256)(128)(2,1)} %param.17) | copy-start | bytes 1156
  6.5 8.6 %copy-start.11 = (bf16[192]{0:T(256)(128)(2,1)S(1)}, bf16[192]{0:T(256)(128)(2,1)}, u32[]{:S(2)}) copy-start(bf16[192]{0:T(256)(128)(2,1)} %param.18) | copy-start | bytes 1156
  6.5 8.6 %copy-start.3 = (bf16[2,192,256]{2,1,0:T(8,128)(2,1)S(1)}, bf16[2,192,256]{2,1,0:T(8,128)(2,1)}, u32[]{:S(2)}) copy-start(bf16[2,192,256]{2,1,0:T(8,128)(2,1)} %latent.1) | copy-start | bytes 589828
  6.5 67.5 %all-gather.2.cloned.1.call-start = ((), (), s32[]{:S(2)}) async-start(), calls=%async_computation | async-start | bytes 5640192 | tf_op jit(solution)/shard_map/all_gather | solution.py:580
  12.1 16.6 %collective-permute-start.1 = (bf16[2,2,192,256]{3,2,1,0:T(8,128)(2,1)S(1)}, bf16[2,2,192,256]{3,2,1,0:T(8,128)(2,1)S(1)}, u32[]{:S(2)}, u32[]{:S(2)}) collective-permute-start(bf16[2,2,192,256]{3,2,1,0:T(8,128)(2,1)S(1)} %copy-done.6), channel_id=1, source_target_pairs={{0,1},{1,0},{2,3},{3,2},{4,5},{5,4},{6,7},{7,6},{8,9},{9,8},{10,11... | collective-permute-start | bytes 1179656 | tf_op jit(solution)/shard_map/ppermute | solution.py:551
  15.2 13.4 %collective-permute-start = (bf16[400,256]{1,0:T(8,128)(2,1)S(1)}, bf16[400,256]{1,0:T(8,128)(2,1)S(1)}, u32[]{:S(2)}, u32[]{:S(2)}) collective-permute-start(bf16[400,256]{1,0:T(8,128)(2,1)S(1)} %fusion.1), channel_id=1, source_target_pairs={{0,1},{1,0},{2,3},{3,2},{4,5},{5,4},{6,7},{7,6},{8,9},{9,8},{10,11... | collective-permute-start | bytes 614408 | tf_op jit(solution)/shard_map/ppermute | solution.py:551
  28.7 2.1 %copy-start = (bf16[3,3,3,192,384]{4,3,2,1,0:T(8,128)(2,1)S(1)}, bf16[3,3,3,192,384]{4,3,2,1,0:T(8,128)(2,1)}, u32[]{:S(2)}) copy-start(bf16[3,3,3,192,384]{4,3,2,1,0:T(8,128)(2,1)} %weights.5) | copy-start | bytes 11943940
  30.8 2.4 %copy-start.1 = (bf16[3,3,3,192,384]{4,3,2,1,0:T(8,128)(2,1)S(1)}, bf16[3,3,3,192,384]{4,3,2,1,0:T(8,128)(2,1)}, u32[]{:S(2)}) copy-start(bf16[3,3,3,192,384]{4,3,2,1,0:T(8,128)(2,1)} %weights.5) | copy-start | bytes 11943940
  30.8 9.7 %copy-start.7 = (bf16[2,2,192,256]{3,2,1,0:T(8,128)(2,1)S(1)}, bf16[2,2,192,256]{3,2,1,0:T(8,128)(2,1)}, u32[]{:S(2)}) copy-start(bf16[2,2,192,256]{3,2,1,0:T(8,128)(2,1)} %own.5) | copy-start | bytes 1179652
  33.2 18.9 %copy-start.2 = (bf16[3,3,3,192,384]{4,3,2,1,0:T(8,128)(2,1)S(1)}, bf16[3,3,3,192,384]{4,3,2,1,0:T(8,128)(2,1)}, u32[]{:S(2)}) copy-start(bf16[3,3,3,192,384]{4,3,2,1,0:T(8,128)(2,1)} %weights.7) | copy-start | bytes 11943940
  35.2 6.8 %collective-permute-start.2 = (bf16[192,256]{1,0:T(8,128)(2,1)S(1)}, bf16[192,256]{1,0:T(8,128)(2,1)S(1)}, u32[]{:S(2)}, u32[]{:S(2)}) collective-permute-start(bf16[192,256]{1,0:T(8,128)(2,1)S(1)} %get-tuple-element.19), channel_id=1, source_target_pairs={{2,4},{4,2},{6,8},{8,6},{10,12},{12,10},{3,5},{5,3},{7,9},{9,7},{1... | collective-permute-start | bytes 294920 | tf_op jit(solution)/shard_map/ppermute | solution.py:560
  35.9 7.3 %collective-permute-start.3 = (bf16[192,256]{1,0:T(8,128)(2,1)S(1)}, bf16[192,256]{1,0:T(8,128)(2,1)S(1)}, u32[]{:S(2)}, u32[]{:S(2)}) collective-permute-start(bf16[192,256]{1,0:T(8,128)(2,1)S(1)} %get-tuple-element.20), channel_id=1, source_target_pairs={{0,2},{2,0},{4,6},{6,4},{8,10},{10,8},{12,14},{14,12},{1,3},{3,1},... | collective-permute-start | bytes 294920 | tf_op jit(solution)/shard_map/ppermute | solution.py:557
  40.5 11.6 %collective-permute-start.5 = (bf16[2,2,192,256]{3,2,1,0:T(8,128)(2,1)S(1)}, bf16[2,2,192,256]{3,2,1,0:T(8,128)(2,1)S(1)}, u32[]{:S(2)}, u32[]{:S(2)}) collective-permute-start(bf16[2,2,192,256]{3,2,1,0:T(8,128)(2,1)S(1)} %copy-done.7), channel_id=1, source_target_pairs={{0,1},{1,0},{2,3},{3,2},{4,5},{5,4},{6,7},{7,6},{8,9},{9,8},{10,11... | collective-permute-start | bytes 1179656 | tf_op jit(solution)/shard_map/ppermute | solution.py:551
  43.2 11.3 %collective-permute-start.4 = (bf16[2,192,256]{2,1,0:T(8,128)(2,1)S(1)}, bf16[2,192,256]{2,1,0:T(8,128)(2,1)S(1)}, u32[]{:S(2)}, u32[]{:S(2)}) collective-permute-start(bf16[2,192,256]{2,1,0:T(8,128)(2,1)S(1)} %pad_maximum_fusion.1.own), channel_id=1, source_target_pairs={{0,1},{1,0},{2,3},{3,2},{4,5},{5,4},{6,7},{7,6},{8,9},{9,8},{10,11... | collective-permute-start | bytes 589832 | tf_op jit(solution)/shard_map/ppermute | solution.py:551
  54.5 9.4 %copy-start.4 = (bf16[2,4,192,256]{3,2,1,0:T(8,128)(2,1)S(1)}, bf16[2,4,192,256]{3,2,1,0:T(8,128)(2,1)}, u32[]{:S(2)}) copy-start(bf16[2,4,192,256]{3,2,1,0:T(8,128)(2,1)} %own_a.1) | copy-start | bytes 2359300
  54.5 9.4 %copy-start.5 = (bf16[2,4,192,256]{3,2,1,0:T(8,128)(2,1)S(1)}, bf16[2,4,192,256]{3,2,1,0:T(8,128)(2,1)}, u32[]{:S(2)}) copy-start(bf16[2,4,192,256]{3,2,1,0:T(8,128)(2,1)} %own_b.1) | copy-start | bytes 2359300
  56.6 5.0 %collective-permute-start.6 = (bf16[192,256]{1,0:T(8,128)(2,1)S(1)}, bf16[192,256]{1,0:T(8,128)(2,1)S(1)}, u32[]{:S(2)}, u32[]{:S(2)}) collective-permute-start(bf16[192,256]{1,0:T(8,128)(2,1)S(1)} %get-tuple-element.22), channel_id=1, source_target_pairs={{0,2},{2,0},{4,6},{6,4},{8,10},{10,8},{12,14},{14,12},{1,3},{3,1},... | collective-permute-start | bytes 294920 | tf_op jit(solution)/shard_map/ppermute | solution.py:557
  57.0 4.5 %collective-permute-start.7 = (bf16[192,256]{1,0:T(8,128)(2,1)S(1)}, bf16[192,256]{1,0:T(8,128)(2,1)S(1)}, u32[]{:S(2)}, u32[]{:S(2)}) collective-permute-start(bf16[192,256]{1,0:T(8,128)(2,1)S(1)} %get-tuple-element.23), channel_id=1, source_target_pairs={{2,4},{4,2},{6,8},{8,6},{10,12},{12,10},{3,5},{5,3},{7,9},{9,7},{1... | collective-permute-start | bytes 294920 | tf_op jit(solution)/shard_map/ppermute | solution.py:560
  62.4 5.7 %collective-permute-start.8 = (bf16[3,192,128]{2,1,0:T(8,128)(2,1)S(1)}, bf16[3,192,128]{2,1,0:T(8,128)(2,1)S(1)}, u32[]{:S(2)}, u32[]{:S(2)}) collective-permute-start(bf16[3,192,128]{2,1,0:T(8,128)(2,1)S(1)} %get-tuple-element.25), channel_id=1, source_target_pairs={{0,1},{1,0},{2,3},{3,2},{4,5},{5,4},{6,7},{7,6},{8,9},{9,8},{10,11... | collective-permute-start | bytes 442376 | tf_op jit(solution)/shard_map/ppermute | solution.py:551
  65.1 8.5 %collective-permute-start.11 = (bf16[192,128]{1,0:T(8,128)(2,1)S(1)}, bf16[192,128]{1,0:T(8,128)(2,1)S(1)}, u32[]{:S(2)}, u32[]{:S(2)}) collective-permute-start(bf16[192,128]{1,0:T(8,128)(2,1)S(1)} %edges.1), channel_id=1, source_target_pairs={{0,1},{1,0},{2,3},{3,2},{4,5},{5,4},{6,7},{7,6},{8,9},{9,8},{10,11... | collective-permute-start | bytes 147464 | tf_op jit(solution)/shard_map/ppermute | solution.py:551
  68.2 20.6 %copy-start.12 = (bf16[192]{0:T(256)(128)(2,1)S(1)}, bf16[192]{0:T(256)(128)(2,1)}, u32[]{:S(2)}) copy-start(bf16[192]{0:T(256)(128)(2,1)} %param.22) | copy-start | bytes 1156
  68.2 20.6 %copy-start.13 = (bf16[192]{0:T(256)(128)(2,1)S(1)}, bf16[192]{0:T(256)(128)(2,1)}, u32[]{:S(2)}) copy-start(bf16[192]{0:T(256)(128)(2,1)} %param.23) | copy-start | bytes 1156
  68.2 20.6 %collective-permute-start.10 = (bf16[5,192,128]{2,1,0:T(8,128)(2,1)S(1)}, bf16[5,192,128]{2,1,0:T(8,128)(2,1)S(1)}, u32[]{:S(2)}, u32[]{:S(2)}) collective-permute-start(bf16[5,192,128]{2,1,0:T(8,128)(2,1)S(1)} %pad_maximum_fusion.one), channel_id=1, source_target_pairs={{0,2},{2,0},{4,6},{6,4},{8,10},{10,8},{12,14},{14,12},{1,3},{3,1},... | collective-permute-start | bytes 737288 | tf_op jit(solution)/shard_map/ppermute | solution.py:557
  72.8 16.1 %collective-permute-start.9 = (bf16[5,192,128]{2,1,0:T(8,128)(2,1)S(1)}, bf16[5,192,128]{2,1,0:T(8,128)(2,1)S(1)}, u32[]{:S(2)}, u32[]{:S(2)}) collective-permute-start(bf16[5,192,128]{2,1,0:T(8,128)(2,1)S(1)} %pad_maximum_fusion.one), channel_id=1, source_target_pairs={{2,4},{4,2},{6,8},{8,6},{10,12},{12,10},{3,5},{5,3},{7,9},{9,7},{1... | collective-permute-start | bytes 737288 | tf_op jit(solution)/shard_map/ppermute | solution.py:560
  74.0 2.5 %copy-start.8 = (bf16[1152,2304]{1,0:T(8,128)(2,1)S(1)}, bf16[1152,2304]{1,0:T(8,128)(2,1)}, u32[]{:S(2)}) copy-start(bf16[1152,2304]{1,0:T(8,128)(2,1)} %all-gather.2.cloned.1.call-done.weights) | copy-start | bytes 15925252
  76.5 24.5 %copy-start.9 = (bf16[1152,2304]{1,0:T(8,128)(2,1)S(1)}, bf16[1152,2304]{1,0:T(8,128)(2,1)}, u32[]{:S(2)}) copy-start(bf16[1152,2304]{1,0:T(8,128)(2,1)} %all-gather.2.cloned.1.call-done.weights) | copy-start | bytes 15925252
  83.4 17.6 %collective-permute-start.12 = (bf16[8,192,128]{2,1,0:T(8,128)(2,1)S(1)}, bf16[8,192,128]{2,1,0:T(8,128)(2,1)S(1)}, u32[]{:S(2)}, u32[]{:S(2)}) collective-permute-start(bf16[8,192,128]{2,1,0:T(8,128)(2,1)S(1)} %get-tuple-element.29), channel_id=1, source_target_pairs={{0,2},{2,0},{4,6},{6,4},{8,10},{10,8},{12,14},{14,12},{1,3},{3,1},... | collective-permute-start | bytes 1179656 | tf_op jit(solution)/shard_map/ppermute | solution.py:557
  88.1 12.9 %collective-permute-start.13 = (bf16[8,192,128]{2,1,0:T(8,128)(2,1)S(1)}, bf16[8,192,128]{2,1,0:T(8,128)(2,1)S(1)}, u32[]{:S(2)}, u32[]{:S(2)}) collective-permute-start(bf16[8,192,128]{2,1,0:T(8,128)(2,1)S(1)} %get-tuple-element.30), channel_id=1, source_target_pairs={{2,4},{4,2},{6,8},{8,6},{10,12},{12,10},{3,5},{5,3},{7,9},{9,7},{1... | collective-permute-start | bytes 1179656 | tf_op jit(solution)/shard_map/ppermute | solution.py:560
Sparse Core Ops, SparseCore 0:
  12.2 61.7 all-gather.1

commit v2 on v1

--- a/solution.py
+++ b/solution.py
@@ -27,19 +27,23 @@
     return lead * rows * lanes * jnp.dtype(shaped.dtype).itemsize
 
 
-def call(body, name, args, outs, scratch, flops):
+def call(body, name, args, outs, scratch, flops, far=(), grant=None):
     moved = sum(size_of(a) for a in args[1:]) + sum(size_of(o) for o in outs)
-    held = moved + sum(size_of(jax.ShapeDtypeStruct(s.shape, s.dtype)) for s in scratch)
+    held = moved + sum(
+        size_of(jax.ShapeDtypeStruct(s.shape, s.dtype)) for s in scratch if len(s.shape) > 1
+    )
     return pl.pallas_call(
         body,
         name=name,
-        in_specs=[SCALAR] + [in_vmem()] * (len(args) - 1),
+        in_specs=[SCALAR]
+        + [in_vmem()] * (len(args) - 1)
+        + [pl.BlockSpec(memory_space=pltpu.HBM)] * len(far),
         out_specs=[in_vmem()] * len(outs),
         out_shape=outs,
         scratch_shapes=scratch,
-        compiler_params=pltpu.CompilerParams(vmem_limit_bytes=held + 4 * MIB),
+        compiler_params=pltpu.CompilerParams(vmem_limit_bytes=grant or held + 4 * MIB),
         cost_estimate=pl.CostEstimate(flops=flops, bytes_accessed=moved, transcendentals=0),
-    )(*args)
+    )(*args, *far)
 
 
 def silu_of(values, scale, gain):
@@ -195,6 +199,42 @@
 
 def one_hot(condition):
     return jnp.where(condition, 1.0, 0.0).astype(BF16)
+
+
+def line_body(place, kernel_a, kernel_b, kernel_r, packet, lined):
+    frames, _, _, share, depth = kernel_a.shape
+    last = frames - 1
+    long = last * 3 * depth
+    for i in range(3):
+        rows = slice(i * share, (i + 1) * share)
+        for j in range(3):
+            for t in range(frames):
+                at = (t * 3 + j) * depth
+                lined[rows, at : at + depth] = kernel_a[t, i, j].astype(F32)
+                at = long + 3 * depth + (j * depth if t == last else (3 + t * 3 + j) * depth)
+                lined[rows, at : at + depth] = kernel_b[t, i, j].astype(F32)
+            at = 2 * long + 6 * depth + 2 * j * depth
+            lined[rows, at : at + 2 * depth] = kernel_r[i, j].astype(F32)
+    lanes = packet.shape[1]
+    total = 2 * long + 12 * depth
+    for view in range(lined.shape[1] // lanes):
+        @pl.when(place[4] == view)
+        def _():
+            stop = min(total, (view + 1) * lanes)
+            packet[:, : stop - view * lanes] = lined[:, view * lanes : stop].astype(BF16)
+
+
+def lined_up(place, kernel_a, kernel_b, kernel_r, lanes, pieces):
+    share = kernel_a.shape[3]
+    return call(
+        line_body,
+        "line",
+        (place, kernel_a, kernel_b, kernel_r),
+        [jax.ShapeDtypeStruct((3 * share, lanes), BF16)],
+        [pltpu.VMEM((3 * share, lanes * pieces), F32)],
+        2 * 3 * share * lanes,
+        grant=63 * MIB,
+    )[0]
 
 
 def edge_body(place, cache_a, cache_b, packet):
@@ -277,14 +317,12 @@
     )
 
 
-def high_sums(total, first, weights, lanes, columns, width, share):
+def high_sums(total, first, held, columns, width, share):
     outs = total.shape[1]
     group = min(2, outs // share)
     for s in range(0, outs // share, group):
         rows = slice(3 * s * share, 3 * (s + group) * share)
-        part = jnp.dot(
-            left_of(weights, 3 * outs, rows, *lanes), columns[:, :width], preferred_element_type=F32
-        )
+        part = jnp.dot(held[rows], columns[:, :width], preferred_element_type=F32)
         for g in range(group):
             for i in range(3):
                 at = 3 * g + i
@@ -293,15 +331,27 @@
                 ]
 
 
-def left_of(weights, height, rows, first, last):
+def fetches(weights, first, held, sems):
+    height, count = held.shape
     lanes = weights.shape[1]
-    parts = []
-    while first < last:
-        piece, start = divmod(first, lanes)
-        stop = min(lanes, start + last - first)
-        parts.append(weights[piece * height + rows.start : piece * height + rows.stop, start:stop])
-        first += stop - start
-    return parts[0] if len(parts) == 1 else jnp.concatenate(parts, axis=1)
+    copies, at = [], 0
+    while at < count:
+        piece, start = divmod(first + at, lanes)
+        size = min(lanes - start, count - at)
+        copies.append(
+            pltpu.make_async_copy(
+                weights.at[piece * height : (piece + 1) * height, start : start + size],
+                held.at[:, at : at + size],
+                sems.at[len(copies)],
+            )
+        )
+        at += size
+    return copies
+
+
+def every(copies, act):
+    for copy in copies:
+        getattr(copy, act)()
 
 
 def kept_lanes(c, width, shape):
@@ -313,15 +363,16 @@
 
 def high_cached_body(
     share, place, own_a, own_b, edge, weights, sums_a, sums_b, red, black, total_a, total_b,
-    columns_a0, columns_a1, columns_b0, columns_b1,
+    columns_a0, columns_a1, columns_b0, columns_b1, held_a, held_b, sems_a, sems_b,
 ):
     frames, rows, depth, width = own_a.shape
     count = total_a.shape[2]
     c, even = place[0], place[3]
+    long = frames * 3 * depth
+    copies = fetches(weights, 0, held_a, sems_a) + fetches(weights, long + 6 * depth, held_b, sems_b)
+    every(copies, "start")
     total_a[...] = jnp.zeros_like(total_a)
     total_b[...] = jnp.zeros_like(total_b)
-    long = frames * 3 * depth
-    second = long + 6 * depth
     lane = lax.broadcasted_iota(jnp.int32, (depth, 128), 1)
 
     def fill(r, columns):
@@ -340,9 +391,10 @@
             spread(columns[1], t * 3 * depth, depth, value, width, False)
 
     def use(r, columns):
-        high_sums(total_a, r, weights, (0, long), columns[0], count, share)
-        high_sums(total_b, r, weights, (second, second + long), columns[1], width, share)
-
+        high_sums(total_a, r, held_a, columns[0], count, share)
+        high_sums(total_b, r, held_b, columns[1], width, share)
+
+    every(copies, "wait")
     in_turn(rows, fill, use, ((columns_a0, columns_b0), (columns_a1, columns_b1)))
     sums_a[...] = total_a[...]
     sums_b[...] = total_b[1 : rows + 1]
@@ -365,7 +417,7 @@
     return call(
         functools.partial(high_cached_body, share),
         "high_cached",
-        (place, own_a, own_b, edge, weights),
+        (place, own_a, own_b, edge),
         [
             jax.ShapeDtypeStruct((rows + 2, depth, count), F32),
             jax.ShapeDtypeStruct((rows, depth, width), F32),
@@ -377,23 +429,26 @@
             pltpu.VMEM((rows + 2, depth, width), F32),
         ]
         + [pltpu.VMEM((frames * 3 * depth, count), BF16)] * 2
-        + [pltpu.VMEM((frames * 3 * depth, width), BF16)] * 2,
+        + [pltpu.VMEM((frames * 3 * depth, width), BF16)] * 2
+        + [pltpu.VMEM((3 * depth, frames * 3 * depth), BF16)] * 2
+        + [pltpu.SemaphoreType.DMA((8,))] * 2,
         2 * frames * 9 * depth * depth * rows * (width + count),
-    )
-
-
-def high_living_body(
-    share, place, one, above, below, gain_a, gain_b, sums_a, sums_b, red, black, weights, decoded,
-    wide, total, total_a, total_b, resampled, columns_r0, columns_r1, columns_0, columns_1,
+        (weights,),
+    )
+
+
+def resample_body(
+    share, place, one, above, below, weights, resampled, wide, total, columns_0, columns_1, held,
+    sems,
 ):
     blocks, half, span = one.shape
     rows = (blocks - 1) // 2
-    high_rows, outs, width = decoded.shape
-    count = sums_a.shape[2]
-    c, first, last, even = place[0], place[1], place[2], place[3]
+    _, outs, count = resampled.shape
+    high_rows, width = 2 * rows, 2 * span
+    c, first, last = place[0], place[1], place[2]
     depth = 2 * half
-    long = 6 * outs
-    keep = kept_lanes(c, width, (outs, count))
+    copies = fetches(weights, 18 * outs, held, sems)
+    every(copies, "start")
 
     lane = lax.broadcasted_iota(jnp.int32, (span + 128, count), 1)
     source = lax.broadcasted_iota(jnp.int32, (span + 128, count), 0)
@@ -421,11 +476,7 @@
         group = min(2, outs // share)
         for s in range(0, outs // share, group):
             picked = slice(3 * s * share, 3 * (s + group) * share)
-            part = jnp.dot(
-                left_of(weights, 3 * outs, picked, 3 * long, 3 * long + 3 * depth),
-                columns[...],
-                preferred_element_type=F32,
-            )
+            part = jnp.dot(held[picked], columns[...], preferred_element_type=F32)
             for g in range(group):
                 at = slice((s + g) * share, (s + g + 1) * share)
                 p0, p1, p2 = (
@@ -436,16 +487,60 @@
                 total[2 * m + 2, at, :] += p0 + p1
                 total[2 * m + 3, at, :] += p0
 
-    buffers = (columns_r0, columns_r1)
+    buffers = (columns_0, columns_1)
     steps = [(one, rows)] + [(above, 0)] + [(below, 2 * rows)]
     steps = [(tile, r, at + r) for tile, at in steps for r in range(rows)]
     fill_low(steps[0][0], steps[0][1], buffers[0])
+    every(copies, "wait")
     for k, (tile, r, at) in enumerate(steps):
         if k + 1 < len(steps):
             fill_low(steps[k + 1][0], steps[k + 1][1], buffers[(k + 1) % 2])
         use_low(at, buffers[k % 2])
 
-    spare = 2 * rows - 1
+    keep = kept_lanes(c, width, (outs, count))
+    for h in range(high_rows + 4):
+        value = jnp.where(keep, total[h + 2 * rows - 1], 0.0).astype(BF16)
+        if h < 2 or h >= high_rows + 2:
+            outside = (first if h < 2 else last) == 1
+            value = jnp.where(outside, jnp.zeros_like(value), value)
+        resampled[h] = value
+
+
+def resample(place, one, above, below, weights, outs, share):
+    blocks, half, span = one.shape
+    rows = (blocks - 1) // 2
+    count = 2 * span + 128
+    depth = 2 * half
+    return call(
+        functools.partial(resample_body, share),
+        "resample",
+        (place, one, above, below),
+        [jax.ShapeDtypeStruct((2 * rows + 4, outs, count), BF16)],
+        [
+            pltpu.VMEM((2 * rows, span + 128, count), BF16),
+            pltpu.VMEM((6 * rows + 2, outs, count), F32),
+        ]
+        + [pltpu.VMEM((3 * depth, count), BF16)] * 2
+        + [pltpu.VMEM((3 * outs, 3 * depth), BF16), pltpu.SemaphoreType.DMA((8,))],
+        2 * 9 * outs * depth * 2 * rows * count,
+        (weights,),
+    )[0]
+
+
+def high_living_body(
+    share, place, resampled, gain_a, gain_b, sums_a, sums_b, red, black, weights, decoded,
+    total_a, total_b, columns_0, columns_1, held_a, held_b, sems_a, sems_b,
+):
+    high_rows, outs, width = decoded.shape
+    count = sums_a.shape[2]
+    c, first, last, even = place[0], place[1], place[2], place[3]
+    long = 6 * outs
+    padded = columns_0.shape[0]
+    copies_a = fetches(weights, long, held_a, sems_a)
+    copies_b = fetches(weights, 2 * long - padded, held_b, sems_b)
+    every(copies_a + copies_b, "start")
+    keep = kept_lanes(c, width, (outs, count))
+
     total_a[...] = jnp.zeros_like(total_a)
     total_a[2 : high_rows + 4] = sums_a[...]
     total_b[...] = jnp.zeros_like(total_b)
@@ -468,18 +563,15 @@
     left_a, left_b = column_of(gain_a[...], 0), column_of(gain_b[...], 0)
 
     def fill_a(h, columns):
-        outside = ((first == 1) & (h < 2)) | ((last == 1) & (h >= high_rows + 2))
-        value = jnp.where(keep, total[h + spare], 0.0).astype(BF16)
-        value = jnp.where(outside, jnp.zeros_like(value), value)
-        resampled[h] = value
-        spread(columns, 0, outs, activated(value.astype(F32), left_a), count, False)
+        value = resampled[h].astype(F32)
+        spread(columns, 0, outs, activated(value, left_a), count, False)
 
     def use_a(h, columns):
-        high_sums(
-            total_a, h, weights, (long, long + columns.shape[0]), columns, count, share
-        )
-
+        high_sums(total_a, h, held_a, columns, count, share)
+
+    every(copies_a, "wait")
     in_turn(high_rows + 4, fill_a, use_a, buffers)
+    every(copies_b, "wait")
     for columns in buffers:
         columns[:pad, :] = jnp.zeros((pad, count), BF16)
 
@@ -490,39 +582,31 @@
         spread(columns, pad, outs, activated(value.astype(F32), left_b), count, False)
 
     def use_b(h, columns):
-        high_sums(
-            total_b, h, weights, (2 * long - columns.shape[0], 2 * long), columns, width, share
-        )
+        high_sums(total_b, h, held_b, columns, width, share)
 
     in_turn(high_rows + 2, fill_b, use_b, buffers)
     for h in range(high_rows):
         decoded[h] = (total_b[h + 2] + resampled[h + 2, :, :width].astype(F32)).astype(BF16)
 
 
-def high_living(
-    place, one, above, below, gain_a, gain_b, sums_a, sums_b, red, black, weights, share
-):
-    blocks, half, span = one.shape
-    rows = (blocks - 1) // 2
+def high_living(place, resampled, gain_a, gain_b, sums_a, sums_b, red, black, weights, share):
     high_rows, outs, width = sums_b.shape
     count = sums_a.shape[2]
-    depth = 2 * half
     padded = -(-3 * outs // 128) * 128
     return call(
         functools.partial(high_living_body, share),
         "high_living",
-        (place, one, above, below, gain_a, gain_b, sums_a, sums_b, red, black, weights),
+        (place, resampled, gain_a, gain_b, sums_a, sums_b, red, black),
         [jax.ShapeDtypeStruct((high_rows, outs, width), BF16)],
         [
-            pltpu.VMEM((2 * rows, span + 128, count), BF16),
-            pltpu.VMEM((6 * rows + 2, outs, count), F32),
             pltpu.VMEM((high_rows + 6, outs, count), F32),
             pltpu.VMEM((high_rows + 4, outs, width), F32),
-            pltpu.VMEM((high_rows + 4, outs, count), BF16),
         ]
-        + [pltpu.VMEM((3 * depth, count), BF16)] * 2
-        + [pltpu.VMEM((padded, count), BF16)] * 2,
-        2 * 27 * outs * outs * high_rows * width + 2 * 9 * outs * depth * high_rows * count,
+        + [pltpu.VMEM((padded, count), BF16)] * 2
+        + [pltpu.VMEM((3 * outs, padded), BF16)] * 2
+        + [pltpu.SemaphoreType.DMA((8,))] * 2,
+        2 * 27 * outs * outs * high_rows * width,
+        (weights,),
     )[0]
 
 
@@ -560,39 +644,47 @@
         return lax.ppermute(value, "rows", blacks)
 
     even = r % 2 == 0
-    place = jnp.stack([c, r == 0, r == row_count - 1, even]).astype(jnp.int32)
-
-    share = kernel_high_a.shape[3]
-
-    def flat(kernel):
-        turned = jnp.transpose(kernel, (1, 3, 0, 2, 4))
-        return turned.reshape(3 * share, -1)
-
-    flat_a, flat_b = flat(kernel_high_a), flat(kernel_high_b)
-    flat_r = flat(resample_kernel[None])
-    outs = kernel_high_a.shape[4]
-    long = 6 * outs
-    lined = jnp.concatenate([flat_a, flat_b[:, long:], flat_b[:, :long], flat_r], axis=1)
-    pieces = lax.axis_size("views")
-    lanes = -(-lined.shape[1] // (128 * pieces)) * 128
-    lined = jnp.pad(lined, ((0, 0), (0, lanes * pieces - lined.shape[1])))
-    mine = lax.dynamic_slice_in_dim(lined, lax.axis_index("views") * lanes, lanes, 1)
-    weights = lax.all_gather(mine, ("views", "rows"), axis=0, tiled=True)
+    view, pieces = lax.axis_index("views"), lax.axis_size("views")
+    place = jnp.stack([c, r == 0, r == row_count - 1, even, view]).astype(jnp.int32)
+
+    share, outs = kernel_high_a.shape[3:]
+    height = 3 * share
+    count = 18 * outs + 3 * resample_kernel.shape[3]
+    lanes = -(-count // (128 * pieces)) * 128
     if share % 8:
-        weights = weights.reshape(pieces, -1, 3, share, lanes).transpose(0, 2, 1, 3, 4)
+
+        def flat(kernel):
+            return jnp.transpose(kernel, (1, 3, 0, 2, 4)).reshape(height, -1)
+
+        flat_a, flat_b = flat(kernel_high_a), flat(kernel_high_b)
+        lined = [flat_a, flat_b[:, 6 * outs :], flat_b[:, : 6 * outs], flat(resample_kernel[None])]
+        lined = jnp.pad(jnp.concatenate(lined, axis=1), ((0, 0), (0, lanes * pieces - count)))
+        mine = lax.dynamic_slice_in_dim(lined, view * lanes, lanes, 1)
+        weights = lax.all_gather(mine, ("views", "rows"), axis=0, tiled=True)
+        weights = weights.reshape(pieces, row_count, 3, share, lanes).transpose(0, 2, 1, 3, 4)
         weights = weights.reshape(-1, lanes)
         share = outs
+    else:
+        with jax.named_scope("prep"):
+            mine = lined_up(
+                place, kernel_high_a, kernel_high_b, resample_kernel, lanes, pieces
+            )
+        weights = lax.all_gather(mine, ("views", "rows"), axis=0, tiled=True)
 
     rows, half, low_width = latent.shape
     gains = jnp.pad(jnp.stack([gain_low_a, gain_low_b]), ((0, 14), (0, 0)))
     sent = jnp.pad(gains, ((0, 0), (0, low_width - half)))
     sent = jnp.concatenate([latent.reshape(rows * half, low_width), sent])
-    got = other_half(sent)
+    with jax.named_scope("e0"):
+        got = other_half(sent)
     other_latent = got[: rows * half].reshape(latent.shape)
     other_gains = got[rows * half :, :half]
-    other_cache_a = other_half(cache_low_a)
-    other_cache_b = other_half(cache_low_b)
-    edge = other_half(edges_of(place, cache_high_a, cache_high_b))
+    with jax.named_scope("e0a"):
+        other_cache_a = other_half(cache_low_a)
+    with jax.named_scope("e0b"):
+        other_cache_b = other_half(cache_low_b)
+    with jax.named_scope("e0s"):
+        edge = other_half(edges_of(place, cache_high_a, cache_high_b))
 
     def low_conv(inputs, other, cached, which, kernel):
         inner, red, black = low_living(
@@ -619,17 +711,21 @@
     sums_a, sums_b, red, black = high_cached(
         place, cache_high_a, cache_high_b, edge, weights, share
     )
+    with jax.named_scope("sumred"):
+        red = by_red(red)
+    with jax.named_scope("sumblack"):
+        black = by_black(black)
+    with jax.named_scope("resampled"):
+        resampled = resample(place, one, above, below, weights, outs, share)
     return high_living(
         place,
-        one,
-        above,
-        below,
+        resampled,
         jnp.pad(gain_high_a[None], ((0, 15), (0, 0))),
         jnp.pad(gain_high_b[None], ((0, 15), (0, 0))),
         sums_a,
         sums_b,
-        by_red(red),
-        by_black(black),
+        red,
+        black,
         weights,
         share,
     )

time: 125 us -> 116 us (0.928)
  waiting for transfers between devices: 40.6 us -> 26.7 us
  starting transfers between devices: 25.5 us -> 28.9 us
  Pallas kernels: 33.9 us -> 36.7 us
  local copies, waits for them, and re-layouts: 10.1 us -> 8.26 us
    ppermute x4, waiting for transfers between devices: 17.1 us -> 8.15 us  [by_red(): return lax.ppermute(value, 'rows', reds)]
    ppermute x6, waiting for transfers between devices: 23 us -> 18.5 us  [other_half(): return lax.ppermute(value, 'chan', swap)]
    ppermute x4, starting transfers between devices: 14.2 us -> 17.7 us  [by_red(): return lax.ppermute(value, 'rows', reds)]
    transpose x3 -> x0, local copies, waits for them, and re-layouts: 3.36 us -> none  [flat(): turned = jnp.transpose(kernel, (1, 3, 0, 2, 4))]
    pallas_call x8 -> x10, Pallas kernels: 33.9 us -> 36.7 us  [call(): pl.pallas_call(body, name=name, in_specs=[SCALAR] + [in_vmem()] * (len(ar...]
    unnamed x29 -> x28, local copies, waits for them, and re-layouts: 4.72 us -> 6.29 us
    another operation x2, local copies, waits for them, and re-layouts: 0.01 us -> 1.32 us  [body(): gains = jnp.pad(jnp.stack([gain_low_a, gain_low_b]), ((0, 14), (0, 0)))]
  transfers between devices with their start and end apart: 15 -> 15, of which waited for: 7 -> 6; matrix products, arithmetic and copies ran while one was open for 0% -> 2% of each run, Pallas kernels for 14% -> 22%
where the time goes in v2:
time: 116 us; the launch traced here: 115 us
  Pallas kernels  36.7 us (32%)
  starting transfers between devices  28.9 us (25%)
  waiting for transfers between devices  26.7 us (23%)
  between operations  13.7 us (12%)
  local copies, waits for them, and re-layouts  8.26 us (7%)
    pallas_call x10, Pallas kernels, call(): pl.pallas_call(body, name=name, in_specs=[SCALAR] + [in_vmem()] * (len(ar...  36.7 us
    ppermute x6, waiting for transfers between devices, other_half(): return lax.ppermute(value, 'chan', swap)  18.5 us
    ppermute x4, starting transfers between devices, by_red(): return lax.ppermute(value, 'rows', reds)  17.7 us
    ppermute x6, starting transfers between devices, other_half(): return lax.ppermute(value, 'chan', swap)  8.39 us
    ppermute x4, waiting for transfers between devices, by_red(): return lax.ppermute(value, 'rows', reds)  8.15 us
    unnamed x28, local copies, waits for them, and re-layouts  6.29 us
    ppermute x4, starting transfers between devices, by_black(): return lax.ppermute(value, 'rows', blacks)  2.84 us
  transfers between devices with their start and end apart: 15, of which 6 were waited for; matrix products, arithmetic and copies ran while one was open for 2% of the time, Pallas kernels for 22%

profile of v2, /device:TPU:0, one launch (start us, length us, event | category | flops | bytes accessed | tf_op | source)
XLA Modules:
  0.0 115.4 jit_solution(8559321141289077016)
XLA Ops:
  7.1 2.0 %line.1 = bf16[72,2304]{1,0:T(8,128)(2,1)} custom-call(s32[5]{0:T(128)} %stack.44.place, bf16[3,3,3,24,192]{4,3,2,1,0:T(8,128)(2,1)} %kernel_a.1, bf16[3,3,3,24,192]{4,3,2,1,0:T(8,128)(2,1)} %kernel_b.1, bf16[3,3,24,384]{3,2,1,0:T(8,128)(2,1)} %kernel_r.1), custom_call_target="tpu_custom_call" | custom-call | flops 331776 | bytes 1474560 | tf_op jit(solution)/shard_map/prep/line/pallas_call | solution.py:35
  9.2 3.1 %collective-permute-start.1 = (bf16[2,2,192,256]{3,2,1,0:T(8,128)(2,1)}, bf16[2,2,192,256]{3,2,1,0:T(8,128)(2,1)S(1)}, u32[]{:S(2)}, u32[]{:S(2)}) collective-permute-start(bf16[2,2,192,256]{3,2,1,0:T(8,128)(2,1)} %own.3), channel_id=1, source_target_pairs={{0,1},{1,0},{2,3},{3,2},{4,5},{5,4},{6,7},{7,6},{8,9},{9,8},{10,11... | collective-permute-start | bytes 1179656 | tf_op jit(solution)/shard_map/e0a/ppermute | solution.py:635
  12.3 0.7 stack.45
  12.9 0.7 stack.46
  13.6 0.9 fusion.1
  14.6 11.4 %collective-permute-done = bf16[400,256]{1,0:T(8,128)(2,1)S(1)} collective-permute-done((bf16[400,256]{1,0:T(8,128)(2,1)S(1)}, bf16[400,256]{1,0:T(8,128)(2,1)S(1)}, u32[]{:S(2)}, u32[]{:S(2)}) %collective-permute-start) | collective-permute-done | bytes 204832 | tf_op jit(solution)/shard_map/e0/ppermute | solution.py:635
  26.0 2.1 %copy-done = bf16[3,3,3,192,384]{4,3,2,1,0:T(8,128)(2,1)S(1)} copy-done((bf16[3,3,3,192,384]{4,3,2,1,0:T(8,128)(2,1)S(1)}, bf16[3,3,3,192,384]{4,3,2,1,0:T(8,128)(2,1)}, u32[]{:S(2)}) %copy-start) | copy-done | bytes 3981336
  28.2 1.0 copy-done.8
  29.8 2.4 %low_cached.2.cached = f32[4,192,256]{2,1,0:T(8,128)S(1)} custom-call(s32[5]{0:T(128)S(1)} %copy-done.10, bf16[2,2,192,256]{3,2,1,0:T(8,128)(2,1)S(1)} %copy-done.8, bf16[2,2,192,256]{3,2,1,0:T(8,128)(2,1)S(1)} %collective-permute-done.1.other, bf16[3,3,3,192,384]{4,3,2,1,0:T(8,128)(2,1)S(1)} %copy-done), custom_call_target="tpu_custom_call" | custom-call | flops 1358954496 | bytes 5554176 | tf_op jit(solution)/shard_map/low_cached/pallas_call | solution.py:35
  32.2 2.0 %low_living.2 = (f32[2,192,256]{2,1,0:T(8,128)S(1)}, bf16[192,256]{1,0:T(8,128)(2,1)S(1)}, bf16[192,256]{1,0:T(8,128)(2,1)S(1)}) custom-call(s32[5]{0:T(128)S(1)} %copy-done.10, bf16[2,192,256]{2,1,0:T(8,128)(2,1)S(1)} %copy-done.5, bf16[2,192,256]{2,1,0:T(8,128)(2,1)S(1)} %bitcast.22, bf16[16,192]{1,0:T(8,128)(2,1)S(1)} %fusion.8.gain, ...), custom_call_target="tpu_custom_call" | custom-call | flops 679477248 | bytes 5767168 | tf_op jit(solution)/shard_map/low_living/pallas_call | solution.py:35
  34.2 0.7 collective-permute-start.2
  34.9 4.6 %collective-permute-start.3 = (bf16[192,256]{1,0:T(8,128)(2,1)S(1)}, bf16[192,256]{1,0:T(8,128)(2,1)S(1)}, u32[]{:S(2)}, u32[]{:S(2)}) collective-permute-start(bf16[192,256]{1,0:T(8,128)(2,1)S(1)} %get-tuple-element.20), channel_id=1, source_target_pairs={{0,2},{2,0},{4,6},{6,4},{8,10},{10,8},{12,14},{14,12},{1,3},{3,1},... | collective-permute-start | bytes 294920 | tf_op jit(solution)/shard_map/ppermute | solution.py:641
  39.5 1.5 %collective-permute-start.5 = (bf16[2,2,192,256]{3,2,1,0:T(8,128)(2,1)S(1)}, bf16[2,2,192,256]{3,2,1,0:T(8,128)(2,1)S(1)}, u32[]{:S(2)}, u32[]{:S(2)}) collective-permute-start(bf16[2,2,192,256]{3,2,1,0:T(8,128)(2,1)S(1)} %copy-done.9), channel_id=1, source_target_pairs={{0,1},{1,0},{2,3},{3,2},{4,5},{5,4},{6,7},{7,6},{8,9},{9,8},{10,11... | collective-permute-start | bytes 1179656 | tf_op jit(solution)/shard_map/e0b/ppermute | solution.py:635
  41.0 3.3 %collective-permute-done.3 = bf16[192,256]{1,0:T(8,128)(2,1)S(1)} collective-permute-done((bf16[192,256]{1,0:T(8,128)(2,1)S(1)}, bf16[192,256]{1,0:T(8,128)(2,1)S(1)}, u32[]{:S(2)}, u32[]{:S(2)}) %collective-permute-start.3) | collective-permute-done | bytes 98336 | tf_op jit(solution)/shard_map/ppermute | solution.py:641
  44.3 1.6 %collective-permute-start.4 = (bf16[2,192,256]{2,1,0:T(8,128)(2,1)S(1)}, bf16[2,192,256]{2,1,0:T(8,128)(2,1)S(1)}, u32[]{:S(2)}, u32[]{:S(2)}) collective-permute-start(bf16[2,192,256]{2,1,0:T(8,128)(2,1)S(1)} %pad_maximum_fusion.1.own), channel_id=1, source_target_pairs={{0,1},{1,0},{2,3},{3,2},{4,5},{5,4},{6,7},{7,6},{8,9},{9,8},{10,11... | collective-permute-start | bytes 589832 | tf_op jit(solution)/shard_map/ppermute | solution.py:635
  45.9 5.3 %collective-permute-done.5.other = bf16[2,2,192,256]{3,2,1,0:T(8,128)(2,1)S(1)} collective-permute-done((bf16[2,2,192,256]{3,2,1,0:T(8,128)(2,1)S(1)}, bf16[2,2,192,256]{3,2,1,0:T(8,128)(2,1)S(1)}, u32[]{:S(2)}, u32[]{:S(2)}) %collective-permute-start.5) | collective-permute-done | bytes 393248 | tf_op jit(solution)/shard_map/e0b/ppermute | solution.py:635
  51.2 2.4 %low_cached.3.cached = f32[4,192,256]{2,1,0:T(8,128)S(1)} custom-call(s32[5]{0:T(128)S(1)} %copy-done.11, bf16[2,2,192,256]{3,2,1,0:T(8,128)(2,1)S(1)} %copy-done.9, bf16[2,2,192,256]{3,2,1,0:T(8,128)(2,1)S(1)} %collective-permute-done.5.other, bf16[3,3,3,192,384]{4,3,2,1,0:T(8,128)(2,1)S(1)} %copy-done.2), custom_call_target="tpu_custom_call" | custom-call | flops 1358954496 | bytes 5554176 | tf_op jit(solution)/shard_map/low_cached/pallas_call | solution.py:35
  53.6 2.0 %low_living.3 = (f32[2,192,256]{2,1,0:T(8,128)S(1)}, bf16[192,256]{1,0:T(8,128)(2,1)S(1)}, bf16[192,256]{1,0:T(8,128)(2,1)S(1)}) custom-call(s32[5]{0:T(128)S(1)} %copy-done.11, bf16[2,192,256]{2,1,0:T(8,128)(2,1)S(1)} %pad_maximum_fusion.1.own, bf16[2,192,256]{2,1,0:T(8,128)(2,1)S(1)} %collective-permute-done.4.other, bf16[16,192]{1,0:T(8,128)(2,1)S(1)} %fusion.8.gain, ...), custom_call_target="tpu_custom_call" | custom-call | flops 679477248 | bytes 5767168 | tf_op jit(solution)/shard_map/low_living/pallas_call | solution.py:35
  56.7 3.6 %collective-permute-done.6.red = bf16[192,256]{1,0:T(8,128)(2,1)S(1)} collective-permute-done((bf16[192,256]{1,0:T(8,128)(2,1)S(1)}, bf16[192,256]{1,0:T(8,128)(2,1)S(1)}, u32[]{:S(2)}, u32[]{:S(2)}) %collective-permute-start.6) | collective-permute-done | bytes 98336 | tf_op jit(solution)/shard_map/ppermute | solution.py:641
  60.3 0.9 close.1
  61.2 1.6 %collective-permute-start.8 = (bf16[3,192,128]{2,1,0:T(8,128)(2,1)S(1)}, bf16[3,192,128]{2,1,0:T(8,128)(2,1)S(1)}, u32[]{:S(2)}, u32[]{:S(2)}) collective-permute-start(bf16[3,192,128]{2,1,0:T(8,128)(2,1)S(1)} %get-tuple-element.25), channel_id=1, source_target_pairs={{0,1},{1,0},{2,3},{3,2},{4,5},{5,4},{6,7},{7,6},{8,9},{9,8},{10,11... | collective-permute-start | bytes 442376 | tf_op jit(solution)/shard_map/ppermute | solution.py:635
  62.7 1.1 edges.1
  64.5 1.9 %collective-permute-done.8 = bf16[3,192,128]{2,1,0:T(8,128)(2,1)S(1)} collective-permute-done((bf16[3,192,128]{2,1,0:T(8,128)(2,1)S(1)}, bf16[3,192,128]{2,1,0:T(8,128)(2,1)S(1)}, u32[]{:S(2)}, u32[]{:S(2)}) %collective-permute-start.8) | collective-permute-done | bytes 147488 | tf_op jit(solution)/shard_map/ppermute | solution.py:635
  66.4 9.3 %collective-permute-start.10 = (bf16[5,192,128]{2,1,0:T(8,128)(2,1)S(1)}, bf16[5,192,128]{2,1,0:T(8,128)(2,1)S(1)}, u32[]{:S(2)}, u32[]{:S(2)}) collective-permute-start(bf16[5,192,128]{2,1,0:T(8,128)(2,1)S(1)} %pad_maximum_fusion.one), channel_id=1, source_target_pairs={{0,2},{2,0},{4,6},{6,4},{8,10},{10,8},{12,14},{14,12},{1,3},{3,1},... | collective-permute-start | bytes 737288 | tf_op jit(solution)/shard_map/ppermute | solution.py:641
  75.7 0.7 collective-permute-start.9
  76.4 2.5 %copy-done.3 = bf16[1152,2304]{1,0:T(8,128)(2,1)S(1)} copy-done((bf16[1152,2304]{1,0:T(8,128)(2,1)S(1)}, bf16[1152,2304]{1,0:T(8,128)(2,1)}, u32[]{:S(2)}) %copy-start.3) | copy-done | bytes 5308440
  78.9 7.0 %high_cached.1 = (f32[6,192,384]{2,1,0:T(8,128)S(1)}, f32[4,192,256]{2,1,0:T(8,128)S(1)}, bf16[8,192,128]{2,1,0:T(8,128)(2,1)S(1)}, bf16[8,192,128]{2,1,0:T(8,128)(2,1)S(1)}) custom-call(s32[5]{0:T(128)S(1)} %copy-done.11, bf16[2,4,192,256]{3,2,1,0:T(8,128)(2,1)S(1)} %copy-done.6, bf16[2,4,192,256]{3,2,1,0:T(8,128)(2,1)S(1)} %copy-done.7, ...), custom_call_target="tpu_custom_call" | custom-call | flops 3397386240 | bytes 4964352 | tf_op jit(solution)/shard_map/high_cached/pallas_call | solution.py:35
  86.0 3.4 %collective-permute-start.12 = (bf16[8,192,128]{2,1,0:T(8,128)(2,1)S(1)}, bf16[8,192,128]{2,1,0:T(8,128)(2,1)S(1)}, u32[]{:S(2)}, u32[]{:S(2)}) collective-permute-start(bf16[8,192,128]{2,1,0:T(8,128)(2,1)S(1)} %get-tuple-element.29), channel_id=1, source_target_pairs={{0,2},{2,0},{4,6},{6,4},{8,10},{10,8},{12,14},{14,12},{1,3},{3,1},... | collective-permute-start | bytes 1179656 | tf_op jit(solution)/shard_map/sumred/ppermute | solution.py:641
  89.3 0.9 collective-permute-start.13
  90.3 7.5 %resample.1.resampled = bf16[8,192,384]{2,1,0:T(8,128)(2,1)S(1)} custom-call(s32[5]{0:T(128)S(1)} %copy-done.11, bf16[5,192,128]{2,1,0:T(8,128)(2,1)S(1)} %pad_maximum_fusion.one, bf16[5,192,128]{2,1,0:T(8,128)(2,1)S(1)} %get-tuple-element.34.above, bf16[5,192,128]{2,1,0:T(8,128)(2,1)S(1)} %get-tuple-element.33.below, bf16[1152,2304]{1,0:T(8,128)(2,1)S(1)} %copy-done.4), custom_call_target="tpu_custom_call" | custom-call | flops 2038431744 | bytes 1916928 | tf_op jit(solution)/shard_map/resampled/resample/pallas_call | solution.py:35
  97.8 1.3 %collective-permute-done.12.red = bf16[8,192,128]{2,1,0:T(8,128)(2,1)S(1)} collective-permute-done((bf16[8,192,128]{2,1,0:T(8,128)(2,1)S(1)}, bf16[8,192,128]{2,1,0:T(8,128)(2,1)S(1)}, u32[]{:S(2)}, u32[]{:S(2)}) %collective-permute-start.12) | collective-permute-done | bytes 393248 | tf_op jit(solution)/shard_map/sumred/ppermute | solution.py:641
  99.1 9.4 %high_living.1 = bf16[4,192,256]{2,1,0:T(8,128)(2,1)} custom-call(s32[5]{0:T(128)S(1)} %copy-done.11, bf16[8,192,384]{2,1,0:T(8,128)(2,1)S(1)} %resample.1.resampled, bf16[16,192]{1,0:T(8,128)(2,1)S(1)} %pad.17.gain_a, bf16[16,192]{1,0:T(8,128)(2,1)S(1)} %pad.18.gain_b, f32[6,192,384]{2,1,0:T(8,128)S(1)} %get-tuple-element.27.sums_a, ...), custom_call_target="tpu_custom_call" | custom-call | flops 2038431744 | bytes 4931584 | tf_op jit(solution)/shard_map/high_living/pallas_call | solution.py:35
  (54 shorter events, 3.3 us)
Async XLA Ops:
  6.5 25.6 %copy-start.5 = (bf16[2,192,256]{2,1,0:T(8,128)(2,1)S(1)}, bf16[2,192,256]{2,1,0:T(8,128)(2,1)}, u32[]{:S(2)}) copy-start(bf16[2,192,256]{2,1,0:T(8,128)(2,1)} %latent.1) | copy-start | bytes 589828
  6.5 69.9 %all-gather.2.cloned.1.call-start = ((), (), s32[]{:S(2)}) async-start(), calls=%async_computation | async-start | bytes 5640192 | tf_op jit(solution)/shard_map/all_gather | solution.py:672
  9.2 16.8 %collective-permute-start.1 = (bf16[2,2,192,256]{3,2,1,0:T(8,128)(2,1)}, bf16[2,2,192,256]{3,2,1,0:T(8,128)(2,1)S(1)}, u32[]{:S(2)}, u32[]{:S(2)}) collective-permute-start(bf16[2,2,192,256]{3,2,1,0:T(8,128)(2,1)} %own.3), channel_id=1, source_target_pairs={{0,1},{1,0},{2,3},{3,2},{4,5},{5,4},{6,7},{7,6},{8,9},{9,8},{10,11... | collective-permute-start | bytes 1179656 | tf_op jit(solution)/shard_map/e0a/ppermute | solution.py:635
  14.6 11.4 %collective-permute-start = (bf16[400,256]{1,0:T(8,128)(2,1)S(1)}, bf16[400,256]{1,0:T(8,128)(2,1)S(1)}, u32[]{:S(2)}, u32[]{:S(2)}) collective-permute-start(bf16[400,256]{1,0:T(8,128)(2,1)S(1)} %fusion.1), channel_id=1, source_target_pairs={{0,1},{1,0},{2,3},{3,2},{4,5},{5,4},{6,7},{7,6},{8,9},{9,8},{10,11... | collective-permute-start | bytes 614408 | tf_op jit(solution)/shard_map/e0/ppermute | solution.py:635
  26.0 2.1 %copy-start = (bf16[3,3,3,192,384]{4,3,2,1,0:T(8,128)(2,1)S(1)}, bf16[3,3,3,192,384]{4,3,2,1,0:T(8,128)(2,1)}, u32[]{:S(2)}) copy-start(bf16[3,3,3,192,384]{4,3,2,1,0:T(8,128)(2,1)} %weights.5) | copy-start | bytes 11943940
  28.2 1.0 copy-start.8
  29.2 0.6 copy-start.10
  29.8 2.4 %copy-start.1 = (bf16[3,3,3,192,384]{4,3,2,1,0:T(8,128)(2,1)S(1)}, bf16[3,3,3,192,384]{4,3,2,1,0:T(8,128)(2,1)}, u32[]{:S(2)}) copy-start(bf16[3,3,3,192,384]{4,3,2,1,0:T(8,128)(2,1)} %weights.5) | copy-start | bytes 11943940
  29.8 9.7 %copy-start.9 = (bf16[2,2,192,256]{3,2,1,0:T(8,128)(2,1)S(1)}, bf16[2,2,192,256]{3,2,1,0:T(8,128)(2,1)}, u32[]{:S(2)}) copy-start(bf16[2,2,192,256]{3,2,1,0:T(8,128)(2,1)} %own.5) | copy-start | bytes 1179652
  32.2 19.0 %copy-start.2 = (bf16[3,3,3,192,384]{4,3,2,1,0:T(8,128)(2,1)S(1)}, bf16[3,3,3,192,384]{4,3,2,1,0:T(8,128)(2,1)}, u32[]{:S(2)}) copy-start(bf16[3,3,3,192,384]{4,3,2,1,0:T(8,128)(2,1)} %weights.7) | copy-start | bytes 11943940
  32.2 19.0 %copy-start.11 = (s32[5]{0:T(128)S(1)}, s32[5]{0:T(128)}, u32[]{:S(2)}) copy-start(s32[5]{0:T(128)} %stack.44.place) | copy-start | bytes 64
  34.2 6.8 %collective-permute-start.2 = (bf16[192,256]{1,0:T(8,128)(2,1)S(1)}, bf16[192,256]{1,0:T(8,128)(2,1)S(1)}, u32[]{:S(2)}, u32[]{:S(2)}) collective-permute-start(bf16[192,256]{1,0:T(8,128)(2,1)S(1)} %get-tuple-element.19), channel_id=1, source_target_pairs={{2,4},{4,2},{6,8},{8,6},{10,12},{12,10},{3,5},{5,3},{7,9},{9,7},{1... | collective-permute-start | bytes 294920 | tf_op jit(solution)/shard_map/ppermute | solution.py:644
  34.9 9.4 %collective-permute-start.3 = (bf16[192,256]{1,0:T(8,128)(2,1)S(1)}, bf16[192,256]{1,0:T(8,128)(2,1)S(1)}, u32[]{:S(2)}, u32[]{:S(2)}) collective-permute-start(bf16[192,256]{1,0:T(8,128)(2,1)S(1)} %get-tuple-element.20), channel_id=1, source_target_pairs={{0,2},{2,0},{4,6},{6,4},{8,10},{10,8},{12,14},{14,12},{1,3},{3,1},... | collective-permute-start | bytes 294920 | tf_op jit(solution)/shard_map/ppermute | solution.py:641
  39.5 11.7 %collective-permute-start.5 = (bf16[2,2,192,256]{3,2,1,0:T(8,128)(2,1)S(1)}, bf16[2,2,192,256]{3,2,1,0:T(8,128)(2,1)S(1)}, u32[]{:S(2)}, u32[]{:S(2)}) collective-permute-start(bf16[2,2,192,256]{3,2,1,0:T(8,128)(2,1)S(1)} %copy-done.9), channel_id=1, source_target_pairs={{0,1},{1,0},{2,3},{3,2},{4,5},{5,4},{6,7},{7,6},{8,9},{9,8},{10,11... | collective-permute-start | bytes 1179656 | tf_op jit(solution)/shard_map/e0b/ppermute | solution.py:635
  44.3 9.2 %collective-permute-start.4 = (bf16[2,192,256]{2,1,0:T(8,128)(2,1)S(1)}, bf16[2,192,256]{2,1,0:T(8,128)(2,1)S(1)}, u32[]{:S(2)}, u32[]{:S(2)}) collective-permute-start(bf16[2,192,256]{2,1,0:T(8,128)(2,1)S(1)} %pad_maximum_fusion.1.own), channel_id=1, source_target_pairs={{0,1},{1,0},{2,3},{3,2},{4,5},{5,4},{6,7},{7,6},{8,9},{9,8},{10,11... | collective-permute-start | bytes 589832 | tf_op jit(solution)/shard_map/ppermute | solution.py:635
  53.5 9.2 %copy-start.6 = (bf16[2,4,192,256]{3,2,1,0:T(8,128)(2,1)S(1)}, bf16[2,4,192,256]{3,2,1,0:T(8,128)(2,1)}, u32[]{:S(2)}) copy-start(bf16[2,4,192,256]{3,2,1,0:T(8,128)(2,1)} %own_a.1) | copy-start | bytes 2359300
  53.5 9.2 %copy-start.7 = (bf16[2,4,192,256]{3,2,1,0:T(8,128)(2,1)S(1)}, bf16[2,4,192,256]{3,2,1,0:T(8,128)(2,1)}, u32[]{:S(2)}) copy-start(bf16[2,4,192,256]{3,2,1,0:T(8,128)(2,1)} %own_b.1) | copy-start | bytes 2359300
  53.5 10.9 %copy-start.12 = (bf16[192]{0:T(256)(128)(2,1)S(1)}, bf16[192]{0:T(256)(128)(2,1)}, u32[]{:S(2)}) copy-start(bf16[192]{0:T(256)(128)(2,1)} %param.22) | copy-start | bytes 1156
  53.6 10.9 %copy-start.13 = (bf16[192]{0:T(256)(128)(2,1)S(1)}, bf16[192]{0:T(256)(128)(2,1)}, u32[]{:S(2)}) copy-start(bf16[192]{0:T(256)(128)(2,1)} %param.23) | copy-start | bytes 1156
  55.6 4.7 %collective-permute-start.6 = (bf16[192,256]{1,0:T(8,128)(2,1)S(1)}, bf16[192,256]{1,0:T(8,128)(2,1)S(1)}, u32[]{:S(2)}, u32[]{:S(2)}) collective-permute-start(bf16[192,256]{1,0:T(8,128)(2,1)S(1)} %get-tuple-element.22), channel_id=1, source_target_pairs={{0,2},{2,0},{4,6},{6,4},{8,10},{10,8},{12,14},{14,12},{1,3},{3,1},... | collective-permute-start | bytes 294920 | tf_op jit(solution)/shard_map/ppermute | solution.py:641
  56.0 4.2 %collective-permute-start.7 = (bf16[192,256]{1,0:T(8,128)(2,1)S(1)}, bf16[192,256]{1,0:T(8,128)(2,1)S(1)}, u32[]{:S(2)}, u32[]{:S(2)}) collective-permute-start(bf16[192,256]{1,0:T(8,128)(2,1)S(1)} %get-tuple-element.23), channel_id=1, source_target_pairs={{2,4},{4,2},{6,8},{8,6},{10,12},{12,10},{3,5},{5,3},{7,9},{9,7},{1... | collective-permute-start | bytes 294920 | tf_op jit(solution)/shard_map/ppermute | solution.py:644
  61.2 5.2 %collective-permute-start.8 = (bf16[3,192,128]{2,1,0:T(8,128)(2,1)S(1)}, bf16[3,192,128]{2,1,0:T(8,128)(2,1)S(1)}, u32[]{:S(2)}, u32[]{:S(2)}) collective-permute-start(bf16[3,192,128]{2,1,0:T(8,128)(2,1)S(1)} %get-tuple-element.25), channel_id=1, source_target_pairs={{0,1},{1,0},{2,3},{3,2},{4,5},{5,4},{6,7},{7,6},{8,9},{9,8},{10,11... | collective-permute-start | bytes 442376 | tf_op jit(solution)/shard_map/ppermute | solution.py:635
  63.8 12.5 %collective-permute-start.11 = (bf16[192,128]{1,0:T(8,128)(2,1)S(1)}, bf16[192,128]{1,0:T(8,128)(2,1)S(1)}, u32[]{:S(2)}, u32[]{:S(2)}) collective-permute-start(bf16[192,128]{1,0:T(8,128)(2,1)S(1)} %edges.1), channel_id=1, source_target_pairs={{0,1},{1,0},{2,3},{3,2},{4,5},{5,4},{6,7},{7,6},{8,9},{9,8},{10,11... | collective-permute-start | bytes 147464 | tf_op jit(solution)/shard_map/e0s/ppermute | solution.py:635
  66.4 23.8 %collective-permute-start.10 = (bf16[5,192,128]{2,1,0:T(8,128)(2,1)S(1)}, bf16[5,192,128]{2,1,0:T(8,128)(2,1)S(1)}, u32[]{:S(2)}, u32[]{:S(2)}) collective-permute-start(bf16[5,192,128]{2,1,0:T(8,128)(2,1)S(1)} %pad_maximum_fusion.one), channel_id=1, source_target_pairs={{0,2},{2,0},{4,6},{6,4},{8,10},{10,8},{12,14},{14,12},{1,3},{3,1},... | collective-permute-start | bytes 737288 | tf_op jit(solution)/shard_map/ppermute | solution.py:641
  75.7 14.5 %collective-permute-start.9 = (bf16[5,192,128]{2,1,0:T(8,128)(2,1)S(1)}, bf16[5,192,128]{2,1,0:T(8,128)(2,1)S(1)}, u32[]{:S(2)}, u32[]{:S(2)}) collective-permute-start(bf16[5,192,128]{2,1,0:T(8,128)(2,1)S(1)} %pad_maximum_fusion.one), channel_id=1, source_target_pairs={{2,4},{4,2},{6,8},{8,6},{10,12},{12,10},{3,5},{5,3},{7,9},{9,7},{1... | collective-permute-start | bytes 737288 | tf_op jit(solution)/shard_map/ppermute | solution.py:644
  76.4 2.5 %copy-start.3 = (bf16[1152,2304]{1,0:T(8,128)(2,1)S(1)}, bf16[1152,2304]{1,0:T(8,128)(2,1)}, u32[]{:S(2)}) copy-start(bf16[1152,2304]{1,0:T(8,128)(2,1)} %all-gather.2.cloned.1.call-done.weights) | copy-start | bytes 15925252
  78.9 11.4 %copy-start.4 = (bf16[1152,2304]{1,0:T(8,128)(2,1)S(1)}, bf16[1152,2304]{1,0:T(8,128)(2,1)}, u32[]{:S(2)}) copy-start(bf16[1152,2304]{1,0:T(8,128)(2,1)} %all-gather.2.cloned.1.call-done.weights) | copy-start | bytes 15925252
  86.0 13.1 %collective-permute-start.12 = (bf16[8,192,128]{2,1,0:T(8,128)(2,1)S(1)}, bf16[8,192,128]{2,1,0:T(8,128)(2,1)S(1)}, u32[]{:S(2)}, u32[]{:S(2)}) collective-permute-start(bf16[8,192,128]{2,1,0:T(8,128)(2,1)S(1)} %get-tuple-element.29), channel_id=1, source_target_pairs={{0,2},{2,0},{4,6},{6,4},{8,10},{10,8},{12,14},{14,12},{1,3},{3,1},... | collective-permute-start | bytes 1179656 | tf_op jit(solution)/shard_map/sumred/ppermute | solution.py:641
  89.3 9.7 %collective-permute-start.13 = (bf16[8,192,128]{2,1,0:T(8,128)(2,1)S(1)}, bf16[8,192,128]{2,1,0:T(8,128)(2,1)S(1)}, u32[]{:S(2)}, u32[]{:S(2)}) collective-permute-start(bf16[8,192,128]{2,1,0:T(8,128)(2,1)S(1)} %get-tuple-element.30), channel_id=1, source_target_pairs={{2,4},{4,2},{6,8},{8,6},{10,12},{12,10},{3,5},{5,3},{7,9},{9,7},{1... | collective-permute-start | bytes 1179656 | tf_op jit(solution)/shard_map/sumblack/ppermute | solution.py:644
Sparse Core Ops, SparseCore 0:
  9.6 61.3 all-gather.1
